TPU v7x, 32 devices: a whole 2x2x4 slice. The times are simulated.
32 devices in a mesh: groups: 2 (over y), gx: 4 (over z), gy: 2 (over x), gz: 2 (over core).
Axes of the slice: x: 2, y: 2, z: 4, core: 2. Of those that a mesh axis runs over, the one named last changes fastest.
Arguments:
- coords: float32 [8, 8, 16, 3, 128], P(('groups', 'gx'), 'gy', 'gz'), parts along dimension 0, may hold values from 0 to 1.1
- charges: float32 [8, 8, 16, 128], P(('groups', 'gx'), 'gy', 'gz'), parts along dimension 0, may hold values from -2 to 2
- atom_types: int32 [8, 8, 16, 128], P(('groups', 'gx'), 'gy', 'gz'), parts along dimension 0, may hold values from 0 to 63
- counts: int32 [8, 8, 16], P(('groups', 'gx'), 'gy', 'gz'), parts along dimension 0, may hold values from 64 to 128
- c6_table: float32 [64, 64], replicated, may hold values from 0.0001 to 0.001
- c12_table: float32 [64, 64], replicated, may hold values from 1e-08 to 1e-07
Outputs:
- forces: float32 [8, 8, 16, 3, 128], P(('groups', 'gx'), 'gy', 'gz'), parts along dimension 0
- energy: float32 [2], P('groups'), parts along dimension 0
There are 2 independent parts, one for each index of `groups`. A program takes and returns all parts, laid end to end along the dimension named above; an argument that names none is the same for every part. Nothing has to cross between parts.
All inputs are finite; a program needn't handle non-finite values.
Results may differ from a plain program's by a relative error of at most 0.0003.
Values sent between devices are 32-bit elements; how exact they have to be, the bound alone decides.
A program may use at most 64 MiB of HBM per device.

v0:
```python
import functools

import jax
import jax.numpy as jnp
from jax import lax
from jax.experimental import pallas as pl
from jax.experimental.pallas import tpu as pltpu
from jax.sharding import PartitionSpec as P

CELL_EDGE = 1.1
SOFTEN = 0.09
ENERGY_UNIT = 0.1
EDGE_V = 1.0 / (1.0 + SOFTEN)
E0 = EDGE_V**0.5
E3 = EDGE_V**3
UNROLL = 8
GROUPS = (
    ((1, -1, -1, 3), (1, 0, -1, 3), (0, 0, 0, 2)),
    ((1, 1, -1, 3), (0, 1, -1, 3)),
)
SELF_ROW = 6


def shifted(block, axis, distance):
    n = lax.axis_size(axis)
    route = [((i - distance) % n, i) for i in range(n)]
    return lax.ppermute(block, axis, route)


def from_both(first, last, axis):
    if lax.axis_size(axis) == 2:
        both = shifted(jnp.stack([first, last]), axis, 1)
        return both[0], both[1]
    return shifted(first, axis, -1), shifted(last, axis, 1)


def ring_sum(value, axis):
    total = value
    for distance in range(1, lax.axis_size(axis)):
        total = total + shifted(value, axis, distance)
    return total


def returned(first, last, energy, axis):
    if lax.axis_size(axis) != 2:
        return (*from_both(first, last, axis), ring_sum(energy, axis))
    slots = energy.shape[-1]
    rows = jnp.stack([first, last]).reshape(-1, slots)
    got = shifted(jnp.concatenate([rows, energy]), axis, 1)
    both = got[:-1].reshape(2, *first.shape)
    return both[0], both[1], energy + got[-1:]


def pair_kernel(cx, cy, cz, nt, scal_ref, type_ref, count_ref, ext_ref, c6_ref, c12_ref,
                force_ref, energy_ref, tcell, table, fa, fb, columns, flat):
    ey = cy + 2
    ez = cz + 2
    slots = 128
    force_ref[...] = jnp.zeros_like(force_ref)
    fa[...] = jnp.zeros_like(fa)
    fb[...] = jnp.zeros_like(fb)
    table[...] = jnp.zeros_like(table)
    c6 = c6_ref[...]
    c12 = c12_ref[...]
    c6 = (0.5 * ENERGY_UNIT) * (c6 + c6.T)
    c12 = (0.5 * ENERGY_UNIT) * (c12 + c12.T)
    both = jnp.concatenate([c12, c6], axis=0)
    high = both.astype(jnp.bfloat16)
    low = (both - high.astype(jnp.float32)).astype(jnp.bfloat16)
    left = jnp.concatenate([high, low], axis=1)
    ids = lax.broadcasted_iota(jnp.int32, (nt, slots), 0).astype(jnp.float32)

    def table_of(xy, carry):
        for z in range(ez):
            row = ext_ref[4, xy, z : z + 1, :]
            hot = (ids == row).astype(jnp.float32).astype(jnp.bfloat16)
            tcell[xy, z] = jnp.dot(
                left, jnp.concatenate([hot, hot], axis=0), preferred_element_type=jnp.float32
            )
        return carry

    lax.fori_loop(1, (cx + 1) * ey, table_of, 0)

    rows = lax.broadcasted_iota(jnp.int32, (8, slots), 0)
    lanes = lax.broadcasted_iota(jnp.int32, (8, slots), 1)
    self_lane = jnp.where(rows == SELF_ROW, lanes, slots)
    wide_lanes = lax.broadcasted_iota(jnp.int32, (slots, slots), 1)
    columns[...] = jnp.zeros_like(columns)

    def cell(c, e_sum):
        x = c // (cy * cz)
        y = (c // cz) % cy
        z = c % cz
        b_rows = []
        for g, runs in enumerate(GROUPS):
            comps = [[], [], [], []]
            r = 0
            for ox, oy, oz, length in runs:
                xy = (x + ox) * ey + y + 1 + oy
                z0 = z + 1 + oz
                for k in range(4):
                    comps[k].append(ext_ref[k, xy, pl.ds(z0, length), :])
                for j in range(length):
                    t = tcell.at[xy, z0 + j]
                    table[g, pl.ds(r, nt, stride=8), :] = t[:nt, :]
                    table[2 + g, pl.ds(r, nt, stride=8), :] = t[nt:, :]
                    r += 1
            if r < 8:
                for k in range(4):
                    comps[k].append(jnp.zeros((8 - r, slots), jnp.float32))
            full = [jnp.concatenate(p, axis=0) for p in comps]
            for k in range(3):
                off = jnp.zeros((8, slots), jnp.float32)
                r = 0
                for ox, oy, oz, length in runs:
                    for j in range(length):
                        o = (ox, oy, oz + j)[k]
                        if o:
                            off = jnp.where(rows == r, jnp.float32(o * CELL_EDGE), off)
                        r += 1
                full[k] = full[k] + off
            b_rows.append(full)
        n_atoms = count_ref[c]

        def fold(step):
            at = pl.ds(pl.multiple_of(step * UNROLL, UNROLL), UNROLL)
            for k in range(3):
                total = fa[k, pl.ds(0, UNROLL, stride=8), :]
                for s in range(1, 8):
                    total = total + fa[k, pl.ds(s, UNROLL, stride=8), :]
                fb[k, at, :] = total

        def atoms(step, carry):
            fold(step)
            acc = [list(carry[0:3]), list(carry[3:6])]
            e_acc = carry[6]
            for uu in range(UNROLL):
                i = step * UNROLL + uu
                at = c * (4 * slots) + i
                xi = scal_ref[at]
                yi = scal_ref[at + slots]
                zi = scal_ref[at + 2 * slots]
                qi = scal_ref[at + 3 * slots]
                ti = pl.multiple_of(type_ref[c * slots + i] * 8, 8)
                mine = None
                for g in range(2):
                    bx, by, bz, bq = b_rows[g]
                    c12p = table[g, pl.ds(ti, 8), :]
                    c6p = table[2 + g, pl.ds(ti, 8), :]
                    dx = bx - xi
                    dy = by - yi
                    dz = bz - zi
                    t = dx * dx + dy * dy + (dz * dz + SOFTEN)
                    s = lax.rsqrt(t)
                    v = s * s
                    z3 = v * v * v
                    w = jnp.maximum((1.0 + SOFTEN) - t, 0.0)
                    if g == 0:
                        w = jnp.where(self_lane > i, w, 0.0)
                    qq = bq * qi
                    cz12 = c12p * z3
                    y1 = cz12 - c6p
                    u = qq * (s - E0) + (z3 - E3) * (y1 + c12p * E3)
                    h = qq * s + (z3 * 6.0) * (y1 + cz12)
                    uw = u * w
                    e_acc = e_acc + uw * w
                    gg = w * (v * h * w) + 4.0 * uw
                    f = [gg * dx, gg * dy, gg * dz]
                    acc[g] = [p + q for p, q in zip(acc[g], f)]
                    mine = f if mine is None else [p + q for p, q in zip(mine, f)]
                for k in range(3):
                    fa[k, pl.ds(uu * 8, 8), :] = mine[k]
            return (*acc[0], *acc[1], e_acc)

        zero = jnp.zeros((8, slots), jnp.float32)
        steps = (n_atoms + UNROLL - 1) // UNROLL
        out = lax.fori_loop(0, steps, atoms, (zero,) * 6 + (e_sum,))
        fold(steps)
        for g, runs in enumerate(GROUPS):
            r = 0
            for ox, oy, oz, length in runs:
                xy = (x + ox) * ey + y + 1 + oy
                for k in range(3):
                    force_ref[k, xy, pl.ds(z + 1 + oz, length), :] += out[3 * g + k][r : r + length]
                r += length
        mine_lane = wide_lanes == c % slots
        for k in range(3):
            summed = jnp.sum(fb[k, pl.ds(UNROLL, slots), :], axis=1, keepdims=True)
            columns[k, c // slots] = jnp.where(mine_lane, summed, columns[k, c // slots])
        return out[6]

    n_cells = cx * cy * cz
    e = lax.fori_loop(0, n_cells, cell, jnp.zeros((8, slots), jnp.float32))
    energy_ref[...] = e
    for k in range(3):
        for part in range(columns.shape[1]):
            flat[pl.ds(part * slots, slots), :] = columns[k, part].T
        for xy in range(cx * cy):
            at = (xy // cy) * ey + xy % cy + 1
            for z in range(cz):
                c = xy * cz + z
                occupied = lanes[:1] < count_ref[c]
                force_ref[k, at, z + 1 : z + 2, :] -= jnp.where(occupied, flat[c : c + 1, :], 0.0)


def on_device(coords, charges, atom_types, counts, c6_table, c12_table):
    cx, cy, cz, _, slots = coords.shape
    nt = c6_table.shape[0]
    occ = jnp.arange(slots, dtype=jnp.int32) < counts[..., None]
    charge = jnp.where(occ, charges, 0.0)
    kind = jnp.where(occ, atom_types, nt)
    local = jnp.concatenate(
        [jnp.moveaxis(coords, 3, 0), charge[None], kind.astype(jnp.float32)[None]], axis=0
    )
    scal = jnp.concatenate([coords, ENERGY_UNIT * charge[..., None, :]], axis=3).reshape(-1)
    up = shifted(local[:, :1], "gx", -1)
    ext = jnp.concatenate([local, up], axis=1)
    above, below = from_both(ext[:, :, :1], ext[:, :, -1:], "gy")
    ext = jnp.concatenate([below, ext, above], axis=2)
    above, below = from_both(ext[:, :, :, :1], ext[:, :, :, -1:], "gz")
    ext = jnp.concatenate([below, ext, above], axis=3)
    parts = (cx * cy * cz + slots - 1) // slots
    ex, ey, ez = cx + 1, cy + 2, cz + 2
    vm = pl.BlockSpec(memory_space=pltpu.VMEM)
    sm = pl.BlockSpec(memory_space=pltpu.SMEM)
    forces, energy = pl.pallas_call(
        functools.partial(pair_kernel, cx, cy, cz, nt),
        out_shape=(
            jax.ShapeDtypeStruct((3, ex * ey, ez, slots), jnp.float32),
            jax.ShapeDtypeStruct((8, slots), jnp.float32),
        ),
        in_specs=[sm, sm, sm, vm, vm, vm],
        out_specs=(vm, vm),
        scratch_shapes=[
            pltpu.VMEM((ex * ey, ez, 2 * nt, slots), jnp.float32),
            pltpu.VMEM((4, (nt + 1) * 8, slots), jnp.float32),
            pltpu.VMEM((3, UNROLL * 8, slots), jnp.float32),
            pltpu.VMEM((3, UNROLL + slots, slots), jnp.float32),
            pltpu.VMEM((3, parts, slots, slots), jnp.float32),
            pltpu.VMEM((parts * slots, slots), jnp.float32),
        ],
        compiler_params=pltpu.CompilerParams(vmem_limit_bytes=48 * 2**20),
    )(scal, kind.reshape(-1), counts.reshape(-1), ext.reshape(5, ex * ey, ez, slots), c6_table, c12_table)
    energy = jnp.sum(energy, axis=0, keepdims=True)
    forces = forces.reshape(3, ex, ey, ez, slots)
    low, high = from_both(forces[:, :, :, :1], forces[:, :, :, -1:], "gz")
    energy = ring_sum(energy, "gx")
    forces = forces[:, :, :, 1:-1].at[:, :, :, -1:].add(low).at[:, :, :, :1].add(high)
    low, high, energy = returned(forces[:, :, :1], forces[:, :, -1:], energy, "gy")
    forces = forces[:, :, 1:-1].at[:, :, -1:].add(low).at[:, :, :1].add(high)
    back = shifted(forces[:, cx:], "gx", 1)
    forces = forces[:, :cx].at[:, :1].add(back)
    energy = jnp.sum(ring_sum(energy, "gz"))
    return jnp.moveaxis(forces, 0, 3), energy.reshape(1)


def solution(mesh):
    return jax.shard_map(
        on_device,
        mesh=mesh,
        in_specs=(
            P(("groups", "gx"), "gy", "gz", None, None),
            P(("groups", "gx"), "gy", "gz", None),
            P(("groups", "gx"), "gy", "gz", None),
            P(("groups", "gx"), "gy", "gz"),
            P(),
            P(),
        ),
        out_specs=(P(("groups", "gx"), "gy", "gz", None, None), P("groups")),
        check_vma=False,
    )
```

profile of v0, /device:TPU:0, one launch (start us, length us, event | category | flops | bytes accessed | tf_op | source)
XLA Modules:
  0.0 110.8 jit_solution(12709060731259322559)
XLA Ops:
  0.6 0.0 copy-start.3
  0.6 0.0 copy-start.2
  0.6 0.8 multiply_bitcast_fusion
  1.5 0.0 copy-done.3
  1.5 0.8 fusion.9
  2.3 0.0 copy-done.2
  2.3 0.1 copy.73
  2.3 0.1 pad_maximum_fusion.3
  2.4 5.1 %collective-permute-start = (f32[5,1,4,8,128]{4,1,0,3,2:T(1,128)S(1)}, f32[5,1,4,8,128]{4,1,0,3,2:T(1,128)S(1)}, u32[]{:S(2)}, u32[]{:S(2)}) collective-permute-start(f32[5,1,4,8,128]{4,1,0,3,2:T(1,128)S(1)} %pad_maximum_fusion.3), channel_id=1, source_target_pairs={{4,0},{8,4},{12,8},{0,12},{5,1},{9,5},{13,9},{1,13},{6,2},{10,6},{... | collective-permute-start | bytes 245768 | tf_op jit(solution)/shard_map/ppermute | solution.py:27
  7.5 2.1 %collective-permute-done = f32[5,1,4,8,128]{4,1,0,3,2:T(1,128)S(1)} collective-permute-done((f32[5,1,4,8,128]{4,1,0,3,2:T(1,128)S(1)}, f32[5,1,4,8,128]{4,1,0,3,2:T(1,128)S(1)}, u32[]{:S(2)}, u32[]{:S(2)}) %collective-permute-start) | collective-permute-done | bytes 81952 | tf_op jit(solution)/shard_map/ppermute | solution.py:27
  9.6 0.2 pad_maximum_fusion.2
  9.8 1.6 %collective-permute-start.1 = (f32[2,5,2,1,8,128]{5,2,1,4,3,0:T(2,128)S(1)}, f32[2,5,2,1,8,128]{5,2,1,4,3,0:T(2,128)S(1)}, u32[]{:S(2)}, u32[]{:S(2)}) collective-permute-start(f32[2,5,2,1,8,128]{5,2,1,4,3,0:T(2,128)S(1)} %pad_maximum_fusion.4), channel_id=1, source_target_pairs={{2,0},{0,2},{3,1},{1,3},{6,4},{4,6},{7,5},{5,7},{10,8},{8,10},{11,... | collective-permute-start | bytes 245768 | tf_op jit(solution)/shard_map/ppermute | solution.py:27
  11.4 0.1 reshape.267.count_ref
  11.4 2.9 %collective-permute-done.1 = f32[2,5,2,1,8,128]{5,2,1,4,3,0:T(2,128)S(1)} collective-permute-done((f32[2,5,2,1,8,128]{5,2,1,4,3,0:T(2,128)S(1)}, f32[2,5,2,1,8,128]{5,2,1,4,3,0:T(2,128)S(1)}, u32[]{:S(2)}, u32[]{:S(2)}) %collective-permute-start.1) | collective-permute-done | bytes 81952 | tf_op jit(solution)/shard_map/ppermute | solution.py:27
  14.3 0.2 pad_maximum_fusion.1
  14.6 0.1 collective-permute-start.2
  14.7 1.2 %collective-permute-done.2 = f32[2,5,2,6,1,128]{5,2,3,1,4,0:T(2,128)S(1)} collective-permute-done((f32[2,5,2,6,1,128]{5,2,3,1,4,0:T(2,128)S(1)}, f32[2,5,2,6,1,128]{5,2,3,1,4,0:T(2,128)S(1)}, u32[]{:S(2)}, u32[]{:S(2)}) %collective-permute-start.2) | collective-permute-done | bytes 61472 | tf_op jit(solution)/shard_map/ppermute | solution.py:27
  16.0 0.0 copy-start
  16.0 0.0 copy-start.1
  16.0 0.1 pad_maximum_fusion.ext_ref
  16.1 0.6 copy-done
  16.7 0.0 copy-done.1
  16.8 72.5 %shard_map.82 = (f32[3,12,10,128]{3,2,1,0:T(8,128)S(1)}, f32[8,128]{1,0:T(8,128)S(1)}) custom-call(f32[16384]{0:T(1024)S(1)} %bitcast.63, s32[4096]{0:T(1024)S(1)} %get-tuple-element.96.type_ref, s32[32]{0:T(128)S(1)} %reshape.267.count_ref, f32[5,12,10,128]{3,2,1,0:T(8,128)S(1)} %pad_maximum_fusion.ext_ref, f32[64,64]{1,0:T(8,128)S(1)} %copy-done, ...), custom_call_target="tpu_custom_call" | custom-call | tf_op jit(solution)/shard_map/pallas_call | solution.py:226
  89.3 0.1 collective-permute-start.4
  89.4 6.7 %collective-permute-start.5 = (f32[1,128]{1,0:T(1,128)S(1)}, f32[1,128]{1,0:T(1,128)S(1)}, u32[]{:S(2)}, u32[]{:S(2)}) collective-permute-start(f32[1,128]{1,0:T(1,128)S(1)} %bitcast.84), channel_id=1, source_target_pairs={{8,0},{12,4},{0,8},{4,12},{9,1},{13,5},{1,9},{5,13},{10,2},{14,6},... | collective-permute-start | bytes 1544 | tf_op jit(solution)/shard_map/ppermute | solution.py:27
  96.0 0.0 collective-permute-start.6
  96.2 0.1 collective-permute-start.3
  96.2 0.1 copy.60
  96.3 0.7 collective-permute-done.4
  97.0 0.6 collective-permute-done.5
  97.6 2.0 %collective-permute-done.6 = f32[1,128]{1,0:T(1,128)S(1)} collective-permute-done((f32[1,128]{1,0:T(1,128)S(1)}, f32[1,128]{1,0:T(1,128)S(1)}, u32[]{:S(2)}, u32[]{:S(2)}) %collective-permute-start.6) | collective-permute-done | bytes 544 | tf_op jit(solution)/shard_map/ppermute | solution.py:27
  99.6 0.0 collective-permute-done.3
  99.8 0.1 collective-permute-start.7
  99.8 4.1 %collective-permute-done.7 = f32[97,128]{1,0:T(8,128)S(1)} collective-permute-done((f32[97,128]{1,0:T(8,128)S(1)}, f32[97,128]{1,0:T(8,128)S(1)}, u32[]{:S(2)}, u32[]{:S(2)}) %collective-permute-start.7) | collective-permute-done | bytes 49696 | tf_op jit(solution)/shard_map/ppermute | solution.py:27
  104.0 0.0 collective-permute-start.9
  104.0 0.1 slice.283
  104.1 0.1 collective-permute-start.8
  104.2 0.9 collective-permute-done.9
  105.1 0.6 add_reduce_fusion
  105.7 4.4 %collective-permute-done.8 = f32[3,1,4,8,128]{4,1,2,0,3:T(1,128)S(1)} collective-permute-done((f32[3,1,4,8,128]{4,1,2,0,3:T(1,128)S(1)}, f32[3,1,4,8,128]{4,1,2,0,3:T(1,128)S(1)}, u32[]{:S(2)}, u32[]{:S(2)}) %collective-permute-start.8) | collective-permute-done | bytes 49184 | tf_op jit(solution)/shard_map/ppermute | solution.py:27
  110.1 0.1 fusion
  110.2 0.6 copy.59
  (28 shorter events, 0.5 us)
Async XLA Ops:
  0.6 0.8 copy-start.3
  0.6 1.6 %copy-start.2 = (f32[1,4,8,3,128]{4,2,3,1,0:T(8,128)S(1)}, f32[1,4,8,3,128]{4,2,3,1,0:T(8,128)}, u32[]{:S(2)}) copy-start(f32[1,4,8,3,128]{4,2,3,1,0:T(8,128)} %param.18) | copy-start | bytes 147460
  2.4 7.2 %collective-permute-start = (f32[5,1,4,8,128]{4,1,0,3,2:T(1,128)S(1)}, f32[5,1,4,8,128]{4,1,0,3,2:T(1,128)S(1)}, u32[]{:S(2)}, u32[]{:S(2)}) collective-permute-start(f32[5,1,4,8,128]{4,1,0,3,2:T(1,128)S(1)} %pad_maximum_fusion.3), channel_id=1, source_target_pairs={{4,0},{8,4},{12,8},{0,12},{5,1},{9,5},{13,9},{1,13},{6,2},{10,6},{... | collective-permute-start | bytes 245768 | tf_op jit(solution)/shard_map/ppermute | solution.py:27
  9.8 4.5 %collective-permute-start.1 = (f32[2,5,2,1,8,128]{5,2,1,4,3,0:T(2,128)S(1)}, f32[2,5,2,1,8,128]{5,2,1,4,3,0:T(2,128)S(1)}, u32[]{:S(2)}, u32[]{:S(2)}) collective-permute-start(f32[2,5,2,1,8,128]{5,2,1,4,3,0:T(2,128)S(1)} %pad_maximum_fusion.4), channel_id=1, source_target_pairs={{2,0},{0,2},{3,1},{1,3},{6,4},{4,6},{7,5},{5,7},{10,8},{8,10},{11,... | collective-permute-start | bytes 245768 | tf_op jit(solution)/shard_map/ppermute | solution.py:27
  14.6 1.3 %collective-permute-start.2 = (f32[2,5,2,6,1,128]{5,2,3,1,4,0:T(2,128)S(1)}, f32[2,5,2,6,1,128]{5,2,3,1,4,0:T(2,128)S(1)}, u32[]{:S(2)}, u32[]{:S(2)}) collective-permute-start(f32[2,5,2,6,1,128]{5,2,3,1,4,0:T(2,128)S(1)} %pad_maximum_fusion.6), channel_id=1, source_target_pairs={{1,0},{0,1},{3,2},{2,3},{5,4},{4,5},{7,6},{6,7},{9,8},{8,9},{11,10... | collective-permute-start | bytes 184328 | tf_op jit(solution)/shard_map/ppermute | solution.py:27
  16.0 0.8 copy-start
  16.0 0.8 copy-start.1
  89.3 7.7 %collective-permute-start.4 = (f32[1,128]{1,0:T(1,128)S(1)}, f32[1,128]{1,0:T(1,128)S(1)}, u32[]{:S(2)}, u32[]{:S(2)}) collective-permute-start(f32[1,128]{1,0:T(1,128)S(1)} %bitcast.83), channel_id=1, source_target_pairs={{12,0},{0,4},{4,8},{8,12},{13,1},{1,5},{5,9},{9,13},{14,2},{2,6},{... | collective-permute-start | bytes 1544 | tf_op jit(solution)/shard_map/ppermute | solution.py:27
  89.4 8.2 %collective-permute-start.5 = (f32[1,128]{1,0:T(1,128)S(1)}, f32[1,128]{1,0:T(1,128)S(1)}, u32[]{:S(2)}, u32[]{:S(2)}) collective-permute-start(f32[1,128]{1,0:T(1,128)S(1)} %bitcast.84), channel_id=1, source_target_pairs={{8,0},{12,4},{0,8},{4,12},{9,1},{13,5},{1,9},{5,13},{10,2},{14,6},... | collective-permute-start | bytes 1544 | tf_op jit(solution)/shard_map/ppermute | solution.py:27
  96.0 3.6 %collective-permute-start.6 = (f32[1,128]{1,0:T(1,128)S(1)}, f32[1,128]{1,0:T(1,128)S(1)}, u32[]{:S(2)}, u32[]{:S(2)}) collective-permute-start(f32[1,128]{1,0:T(1,128)S(1)} %bitcast.85), channel_id=1, source_target_pairs={{4,0},{8,4},{12,8},{0,12},{5,1},{9,5},{13,9},{1,13},{6,2},{10,6},{... | collective-permute-start | bytes 1544 | tf_op jit(solution)/shard_map/ppermute | solution.py:27
  96.2 3.5 %collective-permute-start.3 = (f32[2,3,2,6,1,128]{5,2,3,1,4,0:T(2,128)S(1)}, f32[2,3,2,6,1,128]{5,2,3,1,4,0:T(2,128)S(1)}, u32[]{:S(2)}, u32[]{:S(2)}) collective-permute-start(f32[2,3,2,6,1,128]{5,2,3,1,4,0:T(2,128)S(1)} %pad_maximum_fusion.9), channel_id=1, source_target_pairs={{1,0},{0,1},{3,2},{2,3},{5,4},{4,5},{7,6},{6,7},{9,8},{8,9},{11,10... | collective-permute-start | bytes 110600 | tf_op jit(solution)/shard_map/ppermute | solution.py:27
  99.8 4.2 %collective-permute-start.7 = (f32[97,128]{1,0:T(8,128)S(1)}, f32[97,128]{1,0:T(8,128)S(1)}, u32[]{:S(2)}, u32[]{:S(2)}) collective-permute-start(f32[97,128]{1,0:T(8,128)S(1)} %pad_maximum_fusion.7), channel_id=1, source_target_pairs={{2,0},{0,2},{3,1},{1,3},{6,4},{4,6},{7,5},{5,7},{10,8},{8,10},{11,... | collective-permute-start | bytes 149000 | tf_op jit(solution)/shard_map/ppermute | solution.py:27
  104.0 1.2 %collective-permute-start.9 = (f32[1,128]{1,0:T(1,128)S(1)}, f32[1,128]{1,0:T(1,128)S(1)}, u32[]{:S(2)}, u32[]{:S(2)}) collective-permute-start(f32[1,128]{1,0:T(1,128)S(1)} %slice_add_fusion.3), channel_id=1, source_target_pairs={{1,0},{0,1},{3,2},{2,3},{5,4},{4,5},{7,6},{6,7},{9,8},{8,9},{11,10... | collective-permute-start | bytes 1544 | tf_op jit(solution)/shard_map/ppermute | solution.py:27
  104.1 6.0 %collective-permute-start.8 = (f32[3,1,4,8,128]{4,1,2,0,3:T(1,128)S(1)}, f32[3,1,4,8,128]{4,1,2,0,3:T(1,128)S(1)}, u32[]{:S(2)}, u32[]{:S(2)}) collective-permute-start(f32[3,1,4,8,128]{4,1,2,0,3:T(1,128)S(1)} %slice.283), channel_id=1, source_target_pairs={{12,0},{0,4},{4,8},{8,12},{13,1},{1,5},{5,9},{9,13},{14,2},{2,6},{... | collective-permute-start | bytes 147464 | tf_op jit(solution)/shard_map/ppermute | solution.py:27
where the time goes:
time: 111 us
  Pallas kernels  72.5 us (65%)
  waiting for transfers between devices  18.7 us (17%)
  starting transfers between devices  13.8 us (12%)
  other arithmetic  3.02 us (3%)
  local copies, waits for them, and re-layouts  1.81 us (2%)
    pallas_call x1, Pallas kernels, on_device(): pl.pallas_call(functools.partial(pair_kernel, cx, cy, cz, nt), out_shape=...  72.5 us
    ppermute x10, waiting for transfers between devices, shifted(): return lax.ppermute(block, axis, route)  18.7 us
    ppermute x10, starting transfers between devices, shifted(): return lax.ppermute(block, axis, route)  13.8 us
  transfers between devices with their start and end apart: 10, of which 9 were waited for; matrix products, arithmetic and copies ran while one was open for 1% of the time, Pallas kernels for 0%

commit v1 on v0

v1 whole, which is shorter than its diff:
```python
import functools

import jax
import jax.numpy as jnp
from jax import lax
from jax.experimental import pallas as pl
from jax.experimental.pallas import tpu as pltpu
from jax.sharding import PartitionSpec as P

CELL_EDGE = 1.1
SOFTEN = 0.09
ENERGY_UNIT = 0.1
EDGE_V = 1.0 / (1.0 + SOFTEN)
E0 = EDGE_V**0.5
E3 = EDGE_V**3
E6 = E3 * E3
STRIP = 16
OFFSETS = (
    (0, 0, 1), (0, 1, -1), (0, 1, 0), (0, 1, 1),
    (1, -1, -1), (1, -1, 0), (1, -1, 1),
    (1, 0, -1), (1, 0, 0), (1, 0, 1),
    (1, 1, -1), (1, 1, 0), (1, 1, 1), (0, 0, 0),
)
AXIS_SHIFTS = ((0, 0), (0, 1), (1, -1), (1, 0), (1, 1), (2, -1), (2, 0), (2, 1))
FEATS = 32


def shifted(block, axis, distance):
    n = lax.axis_size(axis)
    route = [((i - distance) % n, i) for i in range(n)]
    return lax.ppermute(block, axis, route)


def from_both(first, last, axis):
    if lax.axis_size(axis) == 2:
        both = shifted(jnp.stack([first, last]), axis, 1)
        return both[0], both[1]
    return shifted(first, axis, -1), shifted(last, axis, 1)


def ring_sum(value, axis):
    total = value
    for distance in range(1, lax.axis_size(axis)):
        total = total + shifted(value, axis, distance)
    return total


def returned(first, last, energy, axis):
    if lax.axis_size(axis) != 2:
        return (*from_both(first, last, axis), ring_sum(energy, axis))
    slots = energy.shape[-1]
    rows = jnp.stack([first, last]).reshape(-1, slots)
    got = shifted(jnp.concatenate([rows, energy]), axis, 1)
    both = got[:-1].reshape(2, *first.shape)
    return both[0], both[1], energy + got[-1:]


def rounded(value):
    return value.astype(jnp.bfloat16).astype(jnp.float32)


def two_parts(value):
    high = rounded(value)
    return high, rounded(value - high)


def three_parts(value):
    high = rounded(value)
    rest = value - high
    middle = rounded(rest)
    return high, middle, rounded(rest - middle)


def pick_rows(rows, choices):
    out = jnp.zeros(rows.shape, jnp.float32)
    for r, value in enumerate(choices):
        if value is not None:
            out = jnp.where(rows == r, value, out)
    return out


def dot(a, b):
    return jnp.dot(a, b, preferred_element_type=jnp.float32)


def pair_kernel(cx, cy, cz, nt, ext_ref, c6_ref, c12_ref, force_ref, energy_ref,
                lh, lx, qb, pos, wc, wk, blocks, qrow, xi, d1, d2, gg, fb, fa):
    ey = cy + 2
    ez = cz + 2
    slots = 128
    n_ext = (cx + 1) * ey * ez
    bf = jnp.bfloat16
    rows = lax.broadcasted_iota(jnp.int32, (8, slots), 0)
    ids = lax.broadcasted_iota(jnp.int32, (nt, slots), 0).astype(jnp.float32)
    c6 = c6_ref[...]
    c12 = c12_ref[...]
    c6 = (0.5 * ENERGY_UNIT) * (c6 + c6.T)
    c12 = (0.5 * ENERGY_UNIT) * (c12 + c12.T)
    both = jnp.concatenate([c12, c6], axis=0)
    high = both.astype(bf)
    low = (both - high.astype(jnp.float32)).astype(bf)
    const = (E3 * c6 - E6 * c12).astype(bf)
    zero_feats = jnp.zeros((nt - FEATS, slots), jnp.float32)

    def positions(f):
        parts = []
        for k in range(3):
            parts.append(two_parts(f[k : k + 1, :] - 0.5 * CELL_EDGE))
        return parts

    def prepare(c, carry):
        f = ext_ref[c]
        hot = (ids == f[4:5, :]).astype(jnp.float32)
        parts = positions(f)
        one = jnp.ones((1, slots), jnp.float32)
        feats = []
        norm = None
        for h, m in parts:
            feats.append(pick_rows(rows, (h, h, m, m, one, one, one)))
            x = h + m
            norm = x * x if norm is None else norm + x * x
        qh, qm = two_parts(f[3:4, :])
        feats.append(pick_rows(rows, (*three_parts(norm), qh, qh, qm, qm)))
        (xh, xm), (yh, ym), (zh, zm) = parts
        pos[c] = pick_rows(rows, (xh, xm, yh, ym, zh, zm, one))
        full = jnp.concatenate([hot, *feats, zero_feats], axis=0).astype(bf)
        lx[c] = full.T
        hot = hot.astype(bf)
        lh[c] = jnp.concatenate([hot, hot], axis=0).T
        qb[c] = jnp.broadcast_to(f[3:4, :], (slots, slots)).T
        return carry

    lax.fori_loop(0, n_ext, prepare, 0)

    def ext_of(a):
        x = a // (cy * cz)
        y = (a // cz) % cy
        z = a % cz
        return (x * ey + y + 1) * ez + z + 1

    def weights(a, carry):
        f = ext_ref[ext_of(a)]
        hot = (ids == f[4:5, :]).astype(jnp.float32).astype(bf)
        th = dot(high, hot).astype(bf)
        tl = dot(low, hot).astype(bf)
        wc[a, :, :slots] = jnp.concatenate([th[:nt], tl[:nt]], axis=0)
        wc[a, :, slots:] = jnp.concatenate([th[nt:], tl[nt:]], axis=0)
        kk = dot(const, hot)
        q = f[3:4, :]
        qh, qm = two_parts((-ENERGY_UNIT * E0) * q)
        qblock = pick_rows(rows, (None, None, None, qh, qm, qh, qm))
        zero = jnp.zeros((8, slots), jnp.float32)
        wk[a] = jnp.concatenate([kk, zero, zero, zero, qblock, zero_feats], axis=0).astype(bf)
        for n, (k, shift) in enumerate(AXIS_SHIFTS):
            h, m = two_parts(f[k : k + 1, :] - (0.5 * CELL_EDGE + shift * CELL_EDGE))
            y = h + m
            sq = y * y
            if k == 0:
                sq = sq + SOFTEN
            h2 = -2.0 * h
            m2 = -2.0 * m
            blocks[a, n] = pick_rows(rows, (h2, m2, h2, m2, *three_parts(sq)))
        qrow[a] = jnp.broadcast_to(ENERGY_UNIT * q, (8, slots))
        group = pos[ext_of(a)]
        xt = jnp.concatenate([group] * (slots // 8), axis=0).T.astype(bf)
        xi[a] = jnp.concatenate([xt, xt], axis=0)
        return carry

    lax.fori_loop(0, cx * cy * cz, weights, 0)

    norm_block = jnp.where(rows < 3, 1.0, 0.0)
    zero_hot = jnp.zeros((nt, slots), bf)
    zero_tail = zero_feats.astype(bf)
    strip_rows = lax.broadcasted_iota(jnp.int32, (STRIP, slots), 0)
    strip_lanes = lax.broadcasted_iota(jnp.int32, (STRIP, slots), 1)

    def neighbour(a, o):
        return ext_of(a) + (o[0] * ey + o[1]) * ez + o[2]

    def forward(a, n):
        o = OFFSETS[n]
        b = neighbour(a, o)
        d1[n % 2] = dot(lh[b], wc[a])
        picks = [AXIS_SHIFTS.index((k, o[k])) for k in range(3)]
        near = jnp.concatenate([blocks[a, p] for p in picks] + [norm_block], axis=0).astype(bf)
        w = jnp.concatenate([zero_hot, near, zero_tail], axis=0)
        d2[n % 2] = dot(lx[b], jnp.concatenate([w, wk[a]], axis=1))

    def compute(a, n, e_acc):
        o = OFFSETS[n]
        b = neighbour(a, o)
        q = qrow[a]
        q = jnp.concatenate([q, q], axis=0)
        own = o == (0, 0, 0)
        for r in range(0, slots, STRIP):
            at = pl.ds(r, STRIP)
            t = d2[n % 2, at, :slots]
            kk = d2[n % 2, at, slots:]
            c12 = d1[n % 2, at, :slots]
            c6 = d1[n % 2, at, slots:]
            charge = qb[b, at, :] * q
            s = lax.rsqrt(t)
            v = s * s
            z3 = v * v * v
            w = jnp.maximum((1.0 + SOFTEN) - t, 0.0)
            if own:
                w = jnp.where(strip_rows + r == strip_lanes, 0.0, w)
            p = charge * s
            m = c12 * z3
            a1 = m - c6
            u = z3 * a1 + p + kk
            h = (z3 * (a1 + m)) * 6.0 + p
            uw = u * w
            e = uw * w
            e_acc = e_acc + (0.5 * e if own else e)
            g = w * (v * w * h) + 4.0 * uw
            gh = g.astype(bf)
            gg[n % 2, at, :slots] = gh
            gg[n % 2, at, slots:] = (g - gh.astype(jnp.float32)).astype(bf)
        return e_acc

    def spread(a, n):
        o = OFFSETS[n]
        b = neighbour(a, o)
        g = gg[n % 2]
        if o != (0, 0, 0):
            out = dot(g, xi[a])
            fb[b, :, 8 * n : 8 * n + 8] = out[:, 8 * n : 8 * n + 8]
        left = pos[b].astype(bf)
        got = dot(left, g)
        fa[n] = got[:, :slots] + got[:, slots:]

    def clear(c, carry):
        fb[c] = jnp.zeros((slots, slots), jnp.float32)
        return carry

    lax.fori_loop(0, n_ext, clear, 0)
    count = len(OFFSETS)

    def shift_sum(parts):
        total = None
        extra = [None, None, None]
        for n, part in parts:
            total = part if total is None else total + part
            for k in range(3):
                s = OFFSETS[n][k]
                if s:
                    term = part if s > 0 else -part
                    extra[k] = term if extra[k] is None else extra[k] + term
        return total, extra

    def cell(a, e_acc):
        forward(a, 0)
        for n in range(count):
            if n + 1 < count:
                forward(a, n + 1)
            e_acc = compute(a, n, e_acc)
            if n:
                spread(a, n - 1)
        spread(a, count - 1)
        total, extra = shift_sum([(n, fa[n]) for n in range(count)])
        x = pos[ext_of(a)]
        s = total[6:7]
        for k in range(3):
            here = x[2 * k : 2 * k + 1] + x[2 * k + 1 : 2 * k + 2]
            moved = total[2 * k : 2 * k + 1] + total[2 * k + 1 : 2 * k + 2] + CELL_EDGE * extra[k][6:7]
            force_ref[ext_of(a), k : k + 1, :] = here * s - moved
        return e_acc

    force_ref[...] = jnp.zeros_like(force_ref)
    e = lax.fori_loop(0, cx * cy * cz, cell, jnp.zeros((STRIP, slots), jnp.float32))
    energy_ref[...] = e[:8] + e[8:]

    def gather(c, carry):
        turned = fb[c].T
        total, extra = shift_sum([(n, turned[8 * n : 8 * n + 8]) for n in range(count - 1)])
        x = pos[c]
        s = total[6:7]
        for k in range(3):
            here = x[2 * k : 2 * k + 1] + x[2 * k + 1 : 2 * k + 2]
            moved = total[2 * k : 2 * k + 1] + total[2 * k + 1 : 2 * k + 2] - CELL_EDGE * extra[k][6:7]
            force_ref[c, k : k + 1, :] += here * s - moved
        return carry

    lax.fori_loop(0, n_ext, gather, 0)


def pair_call(cx, cy, cz, nt, slots, ext, c6_table, c12_table):
    n_ext = (cx + 1) * (cy + 2) * (cz + 2)
    n = cx * cy * cz
    vm = pl.BlockSpec(memory_space=pltpu.VMEM)
    bf = jnp.bfloat16
    return pl.pallas_call(
        functools.partial(pair_kernel, cx, cy, cz, nt),
        out_shape=(
            jax.ShapeDtypeStruct((n_ext, 3, slots), jnp.float32),
            jax.ShapeDtypeStruct((8, slots), jnp.float32),
        ),
        in_specs=[vm, vm, vm],
        out_specs=(vm, vm),
        scratch_shapes=[
            pltpu.VMEM((n_ext, slots, slots), bf),
            pltpu.VMEM((n_ext, slots, slots), bf),
            pltpu.VMEM((n_ext, slots, slots), jnp.float32),
            pltpu.VMEM((n_ext, 8, slots), jnp.float32),
            pltpu.VMEM((n, slots, 2 * slots), bf),
            pltpu.VMEM((n, slots, slots), bf),
            pltpu.VMEM((n, 8, 8, slots), jnp.float32),
            pltpu.VMEM((n, 8, slots), jnp.float32),
            pltpu.VMEM((n, 2 * slots, slots), bf),
            pltpu.VMEM((2, slots, 2 * slots), jnp.float32),
            pltpu.VMEM((2, slots, 2 * slots), jnp.float32),
            pltpu.VMEM((2, slots, 2 * slots), bf),
            pltpu.VMEM((n_ext, slots, slots), jnp.float32),
            pltpu.VMEM((len(OFFSETS), 8, slots), jnp.float32),
        ],
        compiler_params=pltpu.CompilerParams(vmem_limit_bytes=56 * 2**20),
    )(ext, c6_table, c12_table)


def on_device(coords, charges, atom_types, counts, c6_table, c12_table):
    cx, cy, cz, _, slots = coords.shape
    nt = c6_table.shape[0]
    occ = jnp.arange(slots, dtype=jnp.int32) < counts[..., None]
    charge = jnp.where(occ, charges, 0.0)
    kind = jnp.where(occ, atom_types, nt).astype(jnp.float32)
    ext = jnp.concatenate(
        [coords, charge[..., None, :], kind[..., None, :], jnp.zeros((cx, cy, cz, 3, slots), jnp.float32)], axis=3
    )
    up = shifted(ext[:1], "gx", -1)
    ext = jnp.concatenate([ext, up], axis=0)
    above, below = from_both(ext[:, :1], ext[:, -1:], "gy")
    ext = jnp.concatenate([below, ext, above], axis=1)
    above, below = from_both(ext[:, :, :1], ext[:, :, -1:], "gz")
    ext = jnp.concatenate([below, ext, above], axis=2)
    ex, ey, ez = cx + 1, cy + 2, cz + 2
    forces, energy = pair_call(cx, cy, cz, nt, slots, ext.reshape(ex * ey * ez, 8, slots), c6_table, c12_table)
    energy = jnp.sum(energy, axis=0, keepdims=True)
    forces = forces.reshape(ex, ey, ez, 3, slots)
    low, high = from_both(forces[:, :, :1], forces[:, :, -1:], "gz")
    energy = ring_sum(energy, "gx")
    forces = forces[:, :, 1:-1].at[:, :, -1:].add(low).at[:, :, :1].add(high)
    low, high, energy = returned(forces[:, :1], forces[:, -1:], energy, "gy")
    forces = forces[:, 1:-1].at[:, -1:].add(low).at[:, :1].add(high)
    back = shifted(forces[cx:], "gx", 1)
    forces = forces[:cx].at[:1].add(back)
    energy = jnp.sum(ring_sum(energy, "gz"))
    return forces, energy.reshape(1)


def solution(mesh):
    return jax.shard_map(
        on_device,
        mesh=mesh,
        in_specs=(
            P(("groups", "gx"), "gy", "gz", None, None),
            P(("groups", "gx"), "gy", "gz", None),
            P(("groups", "gx"), "gy", "gz", None),
            P(("groups", "gx"), "gy", "gz"),
            P(),
            P(),
        ),
        out_specs=(P(("groups", "gx"), "gy", "gz", None, None), P("groups")),
        check_vma=False,
    )
```

time: 111 us -> 120 us (1.081)
  Pallas kernels: 72.5 us -> 80.2 us
  local copies, waits for them, and re-layouts: 1.81 us -> 3.29 us
    pallas_call x1, Pallas kernels: 72.5 us -> 80.2 us  [pair_call(): pl.pallas_call(functools.partial(pair_kernel, cx, cy, cz, nt), out_shape=...]
  transfers between devices with their start and end apart: 10 -> 10, of which waited for: 9 -> 8; matrix products, arithmetic and copies ran while one was open for 1% -> 1% of each run, Pallas kernels for 0% -> 0%
where the time goes in v1:
time: 120 us
  Pallas kernels  80.2 us (67%)
  waiting for transfers between devices  19.6 us (16%)
  starting transfers between devices  13.4 us (11%)
  local copies, waits for them, and re-layouts  3.29 us (3%)
  other arithmetic  2.62 us (2%)
    pallas_call x1, Pallas kernels, pair_call(): pl.pallas_call(functools.partial(pair_kernel, cx, cy, cz, nt), out_shape=...  80.2 us
    ppermute x10, waiting for transfers between devices, shifted(): return lax.ppermute(block, axis, route)  19.6 us
    ppermute x10, starting transfers between devices, shifted(): return lax.ppermute(block, axis, route)  13.4 us
  transfers between devices with their start and end apart: 10, of which 8 were waited for; matrix products, arithmetic and copies ran while one was open for 1% of the time, Pallas kernels for 0%

profile of v1, /device:TPU:0, one launch (start us, length us, event | category | flops | bytes accessed | tf_op | source)
XLA Modules:
  0.0 120.0 jit_solution(3571726979515114251)
XLA Ops:
  0.6 0.0 copy-start.2
  0.6 0.0 copy-start.3
  0.7 0.8 select_bitcast_fusion
  1.5 0.0 copy-done.2
  1.5 0.0 copy-done.3
  1.5 0.0 copy-start
  1.5 0.1 convert_bitcast_fusion
  1.6 0.7 copy-done
  2.3 5.1 %collective-permute-start = (f32[1,4,8,8,128]{4,2,3,1,0:T(8,128)S(1)}, f32[1,4,8,8,128]{4,2,3,1,0:T(8,128)S(1)}, u32[]{:S(2)}, u32[]{:S(2)}) collective-permute-start(f32[1,4,8,8,128]{4,2,3,1,0:T(8,128)S(1)} %pad_maximum_fusion.1), channel_id=1, source_target_pairs={{4,0},{8,4},{12,8},{0,12},{5,1},{9,5},{13,9},{1,13},{6,2},{10,6},{... | collective-permute-start | bytes 393224 | tf_op jit(solution)/shard_map/ppermute | solution.py:31
  7.4 2.8 %collective-permute-done = f32[1,4,8,8,128]{4,2,3,1,0:T(8,128)S(1)} collective-permute-done((f32[1,4,8,8,128]{4,2,3,1,0:T(8,128)S(1)}, f32[1,4,8,8,128]{4,2,3,1,0:T(8,128)S(1)}, u32[]{:S(2)}, u32[]{:S(2)}) %collective-permute-start) | collective-permute-done | bytes 131104 | tf_op jit(solution)/shard_map/ppermute | solution.py:31
  10.2 1.6 %collective-permute-start.1 = (f32[2,2,1,8,8,128]{5,3,4,1,2,0:T(8,128)S(1)}, f32[2,2,1,8,8,128]{5,3,4,1,2,0:T(8,128)S(1)}, u32[]{:S(2)}, u32[]{:S(2)}) collective-permute-start(f32[2,2,1,8,8,128]{5,3,4,1,2,0:T(8,128)S(1)} %pad_maximum_fusion.2), channel_id=1, source_target_pairs={{2,0},{0,2},{3,1},{1,3},{6,4},{4,6},{7,5},{5,7},{10,8},{8,10},{11,... | collective-permute-start | bytes 393224 | tf_op jit(solution)/shard_map/ppermute | solution.py:31
  11.8 3.5 %collective-permute-done.1 = f32[2,2,1,8,8,128]{5,3,4,1,2,0:T(8,128)S(1)} collective-permute-done((f32[2,2,1,8,8,128]{5,3,4,1,2,0:T(8,128)S(1)}, f32[2,2,1,8,8,128]{5,3,4,1,2,0:T(8,128)S(1)}, u32[]{:S(2)}, u32[]{:S(2)}) %collective-permute-start.1) | collective-permute-done | bytes 131104 | tf_op jit(solution)/shard_map/ppermute | solution.py:31
  15.3 0.1 pad_maximum_fusion.16
  15.3 0.1 collective-permute-start.2
  15.4 1.3 %collective-permute-done.2 = f32[2,2,6,1,8,128]{5,4,2,1,3,0:T(8,128)S(1)} collective-permute-done((f32[2,2,6,1,8,128]{5,4,2,1,3,0:T(8,128)S(1)}, f32[2,2,6,1,8,128]{5,4,2,1,3,0:T(8,128)S(1)}, u32[]{:S(2)}, u32[]{:S(2)}) %collective-permute-start.2) | collective-permute-done | bytes 98336 | tf_op jit(solution)/shard_map/ppermute | solution.py:31
  16.7 0.1 pad_maximum_fusion
  16.9 0.9 copy.33
  17.8 80.2 %shard_map.82 = (f32[120,3,128]{2,1,0:T(4,128)}, f32[8,128]{1,0:T(8,128)}) custom-call(f32[120,8,128]{2,1,0:T(8,128)} %bitcast.66, f32[64,64]{1,0:T(8,128)} %c6_ref.1, f32[64,64]{1,0:T(8,128)} %c12_ref.1), custom_call_target="tpu_custom_call" | custom-call | tf_op jit(solution)/shard_map/pallas_call | solution.py:293
  98.0 0.0 copy-start.1
  98.0 0.7 reduce_sum.18
  98.8 1.5 %collective-permute-start.5 = (f32[1,128]{1,0:T(1,128)S(1)}, f32[1,128]{1,0:T(1,128)S(1)}, u32[]{:S(2)}, u32[]{:S(2)}) collective-permute-start(f32[1,128]{1,0:T(1,128)S(1)} %bitcast.75), channel_id=1, source_target_pairs={{8,0},{12,4},{0,8},{4,12},{9,1},{13,5},{1,9},{5,13},{10,2},{14,6},... | collective-permute-start | bytes 1544 | tf_op jit(solution)/shard_map/ppermute | solution.py:31
  100.2 2.9 %collective-permute-start.6 = (f32[1,128]{1,0:T(1,128)S(1)}, f32[1,128]{1,0:T(1,128)S(1)}, u32[]{:S(2)}, u32[]{:S(2)}) collective-permute-start(f32[1,128]{1,0:T(1,128)S(1)} %bitcast.76), channel_id=1, source_target_pairs={{4,0},{8,4},{12,8},{0,12},{5,1},{9,5},{13,9},{1,13},{6,2},{10,6},{... | collective-permute-start | bytes 1544 | tf_op jit(solution)/shard_map/ppermute | solution.py:31
  103.1 0.5 collective-permute-start.4
  103.6 0.8 fusion.8
  104.4 0.0 copy-done.1
  104.5 0.1 collective-permute-start.3
  104.6 0.0 collective-permute-done.5
  104.6 0.5 collective-permute-done.6
  105.2 3.3 %collective-permute-done.4 = f32[1,128]{1,0:T(1,128)S(1)} collective-permute-done((f32[1,128]{1,0:T(1,128)S(1)}, f32[1,128]{1,0:T(1,128)S(1)}, u32[]{:S(2)}, u32[]{:S(2)}) %collective-permute-start.4) | collective-permute-done | bytes 544 | tf_op jit(solution)/shard_map/ppermute | solution.py:31
  108.5 0.0 collective-permute-done.3
  108.6 1.6 %collective-permute-start.7 = (f32[97,128]{1,0:T(8,128)S(1)}, f32[97,128]{1,0:T(8,128)S(1)}, u32[]{:S(2)}, u32[]{:S(2)}) collective-permute-start(f32[97,128]{1,0:T(8,128)S(1)} %pad_maximum_fusion.9), channel_id=1, source_target_pairs={{2,0},{0,2},{3,1},{1,3},{6,4},{4,6},{7,5},{5,7},{10,8},{8,10},{11,... | collective-permute-start | bytes 149000 | tf_op jit(solution)/shard_map/ppermute | solution.py:31
  110.2 2.6 %collective-permute-done.7 = f32[97,128]{1,0:T(8,128)S(1)} collective-permute-done((f32[97,128]{1,0:T(8,128)S(1)}, f32[97,128]{1,0:T(8,128)S(1)}, u32[]{:S(2)}, u32[]{:S(2)}) %collective-permute-start.7) | collective-permute-done | bytes 49696 | tf_op jit(solution)/shard_map/ppermute | solution.py:31
  112.8 0.1 collective-permute-start.9
  113.0 0.1 collective-permute-start.8
  113.1 1.0 collective-permute-done.9
  114.1 0.6 add_reduce_fusion
  114.7 4.7 %collective-permute-done.8 = f32[1,4,8,3,128]{4,3,2,0,1:T(4,128)S(1)} collective-permute-done((f32[1,4,8,3,128]{4,3,2,0,1:T(4,128)S(1)}, f32[1,4,8,3,128]{4,3,2,0,1:T(4,128)S(1)}, u32[]{:S(2)}, u32[]{:S(2)}) %collective-permute-start.8) | collective-permute-done | bytes 49184 | tf_op jit(solution)/shard_map/ppermute | solution.py:31
  119.4 0.6 copy.39
  (27 shorter events, 0.4 us)
Async XLA Ops:
  0.6 0.8 copy-start.2
  0.6 0.8 copy-start.3
  1.5 0.8 copy-start
  2.3 7.9 %collective-permute-start = (f32[1,4,8,8,128]{4,2,3,1,0:T(8,128)S(1)}, f32[1,4,8,8,128]{4,2,3,1,0:T(8,128)S(1)}, u32[]{:S(2)}, u32[]{:S(2)}) collective-permute-start(f32[1,4,8,8,128]{4,2,3,1,0:T(8,128)S(1)} %pad_maximum_fusion.1), channel_id=1, source_target_pairs={{4,0},{8,4},{12,8},{0,12},{5,1},{9,5},{13,9},{1,13},{6,2},{10,6},{... | collective-permute-start | bytes 393224 | tf_op jit(solution)/shard_map/ppermute | solution.py:31
  10.2 5.0 %collective-permute-start.1 = (f32[2,2,1,8,8,128]{5,3,4,1,2,0:T(8,128)S(1)}, f32[2,2,1,8,8,128]{5,3,4,1,2,0:T(8,128)S(1)}, u32[]{:S(2)}, u32[]{:S(2)}) collective-permute-start(f32[2,2,1,8,8,128]{5,3,4,1,2,0:T(8,128)S(1)} %pad_maximum_fusion.2), channel_id=1, source_target_pairs={{2,0},{0,2},{3,1},{1,3},{6,4},{4,6},{7,5},{5,7},{10,8},{8,10},{11,... | collective-permute-start | bytes 393224 | tf_op jit(solution)/shard_map/ppermute | solution.py:31
  15.3 1.4 %collective-permute-start.2 = (f32[2,2,6,1,8,128]{5,4,2,1,3,0:T(8,128)S(1)}, f32[2,2,6,1,8,128]{5,4,2,1,3,0:T(8,128)S(1)}, u32[]{:S(2)}, u32[]{:S(2)}) collective-permute-start(f32[2,2,6,1,8,128]{5,4,2,1,3,0:T(8,128)S(1)} %pad_maximum_fusion.3), channel_id=1, source_target_pairs={{1,0},{0,1},{3,2},{2,3},{5,4},{4,5},{7,6},{6,7},{9,8},{8,9},{11,10... | collective-permute-start | bytes 294920 | tf_op jit(solution)/shard_map/ppermute | solution.py:31
  98.0 6.4 %copy-start.1 = (f32[120,3,128]{2,1,0:T(4,128)S(1)}, f32[120,3,128]{2,1,0:T(4,128)}, u32[]{:S(2)}) copy-start(f32[120,3,128]{2,1,0:T(4,128)} %get-tuple-element.72) | copy-start | bytes 552964
  98.8 5.9 %collective-permute-start.5 = (f32[1,128]{1,0:T(1,128)S(1)}, f32[1,128]{1,0:T(1,128)S(1)}, u32[]{:S(2)}, u32[]{:S(2)}) collective-permute-start(f32[1,128]{1,0:T(1,128)S(1)} %bitcast.75), channel_id=1, source_target_pairs={{8,0},{12,4},{0,8},{4,12},{9,1},{13,5},{1,9},{5,13},{10,2},{14,6},... | collective-permute-start | bytes 1544 | tf_op jit(solution)/shard_map/ppermute | solution.py:31
  100.2 4.9 %collective-permute-start.6 = (f32[1,128]{1,0:T(1,128)S(1)}, f32[1,128]{1,0:T(1,128)S(1)}, u32[]{:S(2)}, u32[]{:S(2)}) collective-permute-start(f32[1,128]{1,0:T(1,128)S(1)} %bitcast.76), channel_id=1, source_target_pairs={{4,0},{8,4},{12,8},{0,12},{5,1},{9,5},{13,9},{1,13},{6,2},{10,6},{... | collective-permute-start | bytes 1544 | tf_op jit(solution)/shard_map/ppermute | solution.py:31
  103.1 5.4 %collective-permute-start.4 = (f32[1,128]{1,0:T(1,128)S(1)}, f32[1,128]{1,0:T(1,128)S(1)}, u32[]{:S(2)}, u32[]{:S(2)}) collective-permute-start(f32[1,128]{1,0:T(1,128)S(1)} %bitcast.77), channel_id=1, source_target_pairs={{12,0},{0,4},{4,8},{8,12},{13,1},{1,5},{5,9},{9,13},{14,2},{2,6},{... | collective-permute-start | bytes 1544 | tf_op jit(solution)/shard_map/ppermute | solution.py:31
  104.5 3.9 %collective-permute-start.3 = (f32[2,2,6,1,3,128]{5,4,1,2,3,0:T(4,128)S(1)}, f32[2,2,6,1,3,128]{5,4,1,2,3,0:T(4,128)S(1)}, u32[]{:S(2)}, u32[]{:S(2)}) collective-permute-start(f32[2,2,6,1,3,128]{5,4,1,2,3,0:T(4,128)S(1)} %pad_maximum_fusion.17), channel_id=1, source_target_pairs={{1,0},{0,1},{3,2},{2,3},{5,4},{4,5},{7,6},{6,7},{9,8},{8,9},{11,10... | collective-permute-start | bytes 110600 | tf_op jit(solution)/shard_map/ppermute | solution.py:31
  108.6 4.2 %collective-permute-start.7 = (f32[97,128]{1,0:T(8,128)S(1)}, f32[97,128]{1,0:T(8,128)S(1)}, u32[]{:S(2)}, u32[]{:S(2)}) collective-permute-start(f32[97,128]{1,0:T(8,128)S(1)} %pad_maximum_fusion.9), channel_id=1, source_target_pairs={{2,0},{0,2},{3,1},{1,3},{6,4},{4,6},{7,5},{5,7},{10,8},{8,10},{11,... | collective-permute-start | bytes 149000 | tf_op jit(solution)/shard_map/ppermute | solution.py:31
  112.8 1.2 %collective-permute-start.9 = (f32[1,128]{1,0:T(1,128)S(1)}, f32[1,128]{1,0:T(1,128)S(1)}, u32[]{:S(2)}, u32[]{:S(2)}) collective-permute-start(f32[1,128]{1,0:T(1,128)S(1)} %slice_add_fusion.3), channel_id=1, source_target_pairs={{1,0},{0,1},{3,2},{2,3},{5,4},{4,5},{7,6},{6,7},{9,8},{8,9},{11,10... | collective-permute-start | bytes 1544 | tf_op jit(solution)/shard_map/ppermute | solution.py:31
  113.0 6.3 %collective-permute-start.8 = (f32[1,4,8,3,128]{4,3,2,0,1:T(4,128)S(1)}, f32[1,4,8,3,128]{4,3,2,0,1:T(4,128)S(1)}, u32[]{:S(2)}, u32[]{:S(2)}) collective-permute-start(f32[1,4,8,3,128]{4,3,2,0,1:T(4,128)S(1)} %slice.279), channel_id=1, source_target_pairs={{12,0},{0,4},{4,8},{8,12},{13,1},{1,5},{5,9},{9,13},{14,2},{2,6},{... | collective-permute-start | bytes 147464 | tf_op jit(solution)/shard_map/ppermute | solution.py:31

commit v2 on v1

v2 whole, which is shorter than its diff:
```python
import functools

import jax
import jax.numpy as jnp
from jax import lax
from jax.experimental import pallas as pl
from jax.experimental.pallas import tpu as pltpu
from jax.sharding import PartitionSpec as P

CELL_EDGE = 1.1
SOFTEN = 0.09
ENERGY_UNIT = 0.1
EDGE_V = 1.0 / (1.0 + SOFTEN)
E0 = EDGE_V**0.5
E3 = EDGE_V**3
STRIP = 16
GROUP = 2
OFFSETS = (
    (0, 0, 1), (0, 1, -1), (0, 1, 0), (0, 1, 1),
    (1, -1, -1), (1, -1, 0), (1, -1, 1),
    (1, 0, -1), (1, 0, 0), (1, 0, 1),
    (1, 1, -1), (1, 1, 0), (1, 1, 1), (0, 0, 0),
)
AXIS_SHIFTS = ((0, 0), (0, 1), (1, -1), (1, 0), (1, 1), (2, -1), (2, 0), (2, 1))
FEATS = 32


def rounded(value):
    return value.astype(jnp.bfloat16).astype(jnp.float32)


def two_parts(value):
    high = rounded(value)
    return high, rounded(value - high)


def three_parts(value):
    high = rounded(value)
    rest = value - high
    middle = rounded(rest)
    return high, middle, rounded(rest - middle)


def pick_rows(rows, choices):
    out = jnp.zeros(rows.shape, jnp.float32)
    for r, value in enumerate(choices):
        if value is not None:
            out = jnp.where(rows == r, value, out)
    return out


def dot(a, b):
    return jnp.dot(a, b, preferred_element_type=jnp.float32)


def unroll_of(count, most):
    return max(u for u in range(1, most + 1) if count % u == 0)


def unrolled(count, most, body):
    u = unroll_of(count, most)

    def step(i, carry):
        for k in range(u):
            body(i * u + k)
        return carry

    lax.fori_loop(0, count // u, step, 0)


def pair_kernel(cx, cy, cz, nt, ext_ref, c6_ref, c12_ref, force_ref, energy_ref,
                lh, lc, pos, wc, blocks, xi, gg, fb, fa):
    ey = cy + 2
    ez = cz + 2
    slots = 128
    n_ext = (cx + 1) * ey * ez
    n_own = cx * cy * cz
    bf = jnp.bfloat16
    rows = lax.broadcasted_iota(jnp.int32, (8, slots), 0)
    ids = lax.broadcasted_iota(jnp.int32, (nt, slots), 0).astype(jnp.float32)
    c6 = c6_ref[...]
    c12 = c12_ref[...]
    c12 = (0.5 * ENERGY_UNIT) * (c12 + c12.T)
    c6 = (0.5 * ENERGY_UNIT) * (c6 + c6.T) - (2.0 * E3) * c12
    both = jnp.concatenate([c12, c6], axis=0)
    high = both.astype(bf)
    low = (both - high.astype(jnp.float32)).astype(bf)
    one = jnp.ones((1, slots), jnp.float32)

    def prepare(c):
        f = ext_ref[c]
        hot = (ids == f[4:5, :]).astype(jnp.float32).astype(bf)
        parts = [two_parts(f[k : k + 1, :] - 0.5 * CELL_EDGE) for k in range(3)]
        feats = []
        norm = None
        for h, m in parts:
            feats.append(pick_rows(rows, (h, h, m, m, one, one, one)))
            x = h + m
            norm = x * x if norm is None else norm + x * x
        qh, qm = two_parts(f[3:4, :])
        feats.append(pick_rows(rows, (*three_parts(norm), qh, qh, qm, qm)))
        (xh, xm), (yh, ym), (zh, zm) = parts
        pos[c] = pick_rows(rows, (xh, xm, yh, ym, zh, zm, one))
        lc[c] = jnp.concatenate(feats, axis=0).astype(bf).T
        lh[c] = jnp.concatenate([hot, hot], axis=0).T

    unrolled(n_ext, 5, prepare)

    def ext_of(a):
        x = a // (cy * cz)
        y = (a // cz) % cy
        z = a % cz
        return (x * ey + y + 1) * ez + z + 1

    def weights(a):
        f = ext_ref[ext_of(a)]
        hot = (ids == f[4:5, :]).astype(jnp.float32).astype(bf)
        th = dot(high, hot).astype(bf)
        tl = dot(low, hot).astype(bf)
        wc[a, :, :slots] = jnp.concatenate([th[:nt], tl[:nt]], axis=0)
        wc[a, :, slots:] = jnp.concatenate([th[nt:], tl[nt:]], axis=0)
        for n, (k, shift) in enumerate(AXIS_SHIFTS):
            h, m = two_parts(f[k : k + 1, :] - (0.5 * CELL_EDGE + shift * CELL_EDGE))
            y = h + m
            sq = y * y
            if k == 0:
                sq = sq + SOFTEN
            h2 = -2.0 * h
            m2 = -2.0 * m
            blocks[a, n] = pick_rows(rows, (h2, m2, h2, m2, *three_parts(sq)))
        qh, qm = two_parts(ENERGY_UNIT * f[3:4, :])
        blocks[a, len(AXIS_SHIFTS)] = pick_rows(rows, (None, None, None, qh, qm, qh, qm))
        group = pos[ext_of(a)]
        xt = jnp.concatenate([group] * (slots // 8), axis=0).astype(bf).T
        xi[a] = jnp.concatenate([xt, xt], axis=0)

    unrolled(n_own, 4, weights)

    norm_block = jnp.where(rows < 3, 1.0, 0.0)
    zero_block = jnp.zeros((8, slots), jnp.float32)
    strip_rows = lax.broadcasted_iota(jnp.int32, (STRIP, slots), 0)
    strip_lanes = lax.broadcasted_iota(jnp.int32, (STRIP, slots), 1)
    count = len(OFFSETS)
    items = count // GROUP

    def neighbour(a, n):
        o = OFFSETS[n]
        return ext_of(a) + (o[0] * ey + o[1]) * ez + o[2]

    def forward(a, i):
        members = range(i * GROUP, (i + 1) * GROUP)
        v1 = dot(jnp.concatenate([lh[neighbour(a, n)] for n in members], axis=0), wc[a])
        v2 = []
        charge = jnp.concatenate([zero_block] * 3 + [blocks[a, len(AXIS_SHIFTS)]], axis=0).astype(bf)
        for j, n in enumerate(members):
            picks = [AXIS_SHIFTS.index((k, OFFSETS[n][k])) for k in range(3)]
            near = jnp.concatenate([blocks[a, p] for p in picks] + [norm_block], axis=0).astype(bf)
            v2.append(dot(lc[neighbour(a, n)], jnp.concatenate([near, charge], axis=1)))
        return v1, v2

    def compute(i, e_acc, vals):
        v1, v2 = vals

        for j in range(GROUP):
            own = OFFSETS[i * GROUP + j] == (0, 0, 0)
            for r in range(0, slots, STRIP):
                at = pl.ds(j * slots + r, STRIP)
                t = v2[j][r:r+STRIP, :slots]
                charge = v2[j][r:r+STRIP, slots:]
                c12 = v1[j*slots+r:j*slots+r+STRIP, :slots]
                c6 = v1[j*slots+r:j*slots+r+STRIP, slots:]
                s = lax.rsqrt(t)
                v = s * s
                z3 = v * v * v
                w = jnp.maximum((1.0 + SOFTEN) - t, 0.0)
                if own:
                    w = jnp.where(strip_rows + r == strip_lanes, 0.0, w)
                y = z3 - E3
                m = c12 * y
                b1 = m - c6
                p = charge * s
                u = y * b1 + charge * (s - E0)
                h = (z3 * (b1 + m)) * 6.0 + p
                uw = u * w
                e = uw * w
                e_acc = e_acc + (0.5 * e if own else e)
                g = w * (v * w * h) + 4.0 * uw
                gh = g.astype(bf)
                gg[i, at, :slots] = gh
                gg[i, at, slots:] = (g - gh.astype(jnp.float32)).astype(bf)
        return e_acc

    def spread(a, i):
        out = dot(gg[i], xi[a])
        for j in range(GROUP):
            n = i * GROUP + j
            b = neighbour(a, n)
            if OFFSETS[n] != (0, 0, 0):
                fb[b, :, 8 * n : 8 * n + 8] = out[j * slots : (j + 1) * slots, 8 * n : 8 * n + 8]
            got = dot(pos[b].astype(bf), gg[i, pl.ds(j * slots, slots), :])
            fa[n] = got[:, :slots] + got[:, slots:]

    def clear(c):
        fb[c] = jnp.zeros((slots, slots), jnp.float32)

    unrolled(n_ext, 2, clear)

    def shift_sum(parts):
        total = None
        extra = [None, None, None]
        for n, part in parts:
            total = part if total is None else total + part
            for k in range(3):
                s = OFFSETS[n][k]
                if s:
                    term = part if s > 0 else -part
                    extra[k] = term if extra[k] is None else extra[k] + term
        return total, extra

    def finish(a):
        total, extra = shift_sum([(n, fa[n]) for n in range(count)])
        x = pos[ext_of(a)]
        s = total[6:7]
        for k in range(3):
            here = x[2 * k : 2 * k + 1] + x[2 * k + 1 : 2 * k + 2]
            moved = total[2 * k : 2 * k + 1] + total[2 * k + 1 : 2 * k + 2] + CELL_EDGE * extra[k][6:7]
            force_ref[ext_of(a), k : k + 1, :] = here * s - moved

    def cell(a, e_acc):
        before = jnp.maximum(a - 1, 0)
        after = jnp.minimum(a + 1, n_own - 1)
        vals = forward(a, 0)
        for i in range(items):
            nxt = forward(a, i + 1) if i + 1 < items else None
            e_acc = compute(i, e_acc, vals)
            vals = nxt
            if i:
                spread(a, i - 1)
            else:
                spread(before, items - 1)
                finish(before)
        return e_acc

    force_ref[...] = jnp.zeros_like(force_ref)
    gg[items - 1] = jnp.zeros_like(gg[items - 1])
    fa[...] = jnp.zeros_like(fa)
    e = lax.fori_loop(0, n_own, cell, jnp.zeros((STRIP, slots), jnp.float32))
    spread(n_own - 1, items - 1)
    finish(n_own - 1)
    energy_ref[...] = e[:8] + e[8:]

    def gather(c):
        turned = fb[c].T
        total, extra = shift_sum([(n, turned[8 * n : 8 * n + 8]) for n in range(count - 1)])
        x = pos[c]
        s = total[6:7]
        for k in range(3):
            here = x[2 * k : 2 * k + 1] + x[2 * k + 1 : 2 * k + 2]
            moved = total[2 * k : 2 * k + 1] + total[2 * k + 1 : 2 * k + 2] - CELL_EDGE * extra[k][6:7]
            force_ref[c, k : k + 1, :] += here * s - moved

    unrolled(n_ext, 5, gather)


def pair_call(cx, cy, cz, nt, slots, ext, c6_table, c12_table):
    n_ext = (cx + 1) * (cy + 2) * (cz + 2)
    n = cx * cy * cz
    vm = pl.BlockSpec(memory_space=pltpu.VMEM)
    bf = jnp.bfloat16
    items = len(OFFSETS) // GROUP
    return pl.pallas_call(
        functools.partial(pair_kernel, cx, cy, cz, nt),
        out_shape=(
            jax.ShapeDtypeStruct((n_ext, 3, slots), jnp.float32),
            jax.ShapeDtypeStruct((8, slots), jnp.float32),
        ),
        in_specs=[vm, vm, vm],
        out_specs=(vm, vm),
        scratch_shapes=[
            pltpu.VMEM((n_ext, slots, slots), bf),
            pltpu.VMEM((n_ext, slots, FEATS), bf),
            pltpu.VMEM((n_ext, 8, slots), jnp.float32),
            pltpu.VMEM((n, slots, 2 * slots), bf),
            pltpu.VMEM((n, len(AXIS_SHIFTS) + 1, 8, slots), jnp.float32),
            pltpu.VMEM((n, 2 * slots, slots), bf),
            pltpu.VMEM((items, GROUP * slots, 2 * slots), bf),
            pltpu.VMEM((n_ext, slots, slots), jnp.float32),
            pltpu.VMEM((len(OFFSETS), 8, slots), jnp.float32),
        ],
        compiler_params=pltpu.CompilerParams(vmem_limit_bytes=56 * 2**20),
    )(ext, c6_table, c12_table)


MESH = pl.DeviceIdType.MESH
AXES = ("gx", "gy", "gz")
REGIONS = (
    (1, 0, 0), (1, 1, 0), (1, -1, 0), (1, 0, 1), (1, 0, -1), (1, 1, 1), (1, 1, -1), (1, -1, 1), (1, -1, -1),
    (0, 1, 0), (0, 1, 1), (0, 1, -1), (0, 0, 1), (0, 0, -1),
)


def sizes():
    return tuple(lax.axis_size(name) for name in AXES)


def device_at(step):
    return {name: lax.rem(lax.axis_index(name) + d % n, n) for name, d, n in zip(AXES, step, sizes())}


def wrapped(step):
    return tuple(d % n for d, n in zip(step, sizes()))


def meet(steps):
    barrier = pltpu.get_barrier_semaphore()
    near = {wrapped(s) for s in steps} | {wrapped([-d for d in s]) for s in steps}
    near = sorted(near - {(0, 0, 0)})
    for step in near:
        pl.semaphore_signal(barrier, inc=1, device_id=device_at(step), device_id_type=MESH)
    pl.semaphore_wait(barrier, len(near))


def halo_at(region, size):
    cx, cy, cz = size
    x = pl.ds(cx, 1) if region[0] else pl.ds(0, cx)
    y = {-1: pl.ds(0, 1), 0: pl.ds(1, cy), 1: pl.ds(cy + 1, 1)}[region[1]]
    z = {-1: pl.ds(0, 1), 0: pl.ds(1, cz), 1: pl.ds(cz + 1, 1)}[region[2]]
    return x, y, z


def edge_at(region, size):
    cx, cy, cz = size
    x = pl.ds(0, 1) if region[0] else pl.ds(0, cx)
    y = {-1: pl.ds(cy - 1, 1), 0: pl.ds(0, cy), 1: pl.ds(0, 1)}[region[1]]
    z = {-1: pl.ds(cz - 1, 1), 0: pl.ds(0, cz), 1: pl.ds(0, 1)}[region[2]]
    return x, y, z


def halo_kernel(size, local_ref, ext_ref, send_sem, recv_sem):
    cx, cy, cz = size
    ext_ref[pl.ds(0, cx), pl.ds(1, cy), pl.ds(1, cz)] = local_ref[...]
    ext_ref[0, 0] = jnp.zeros_like(ext_ref[0, 0])
    meet(REGIONS)
    copies = []
    for n, region in enumerate(REGIONS):
        copy = pltpu.make_async_remote_copy(
            src_ref=local_ref.at[edge_at(region, size)],
            dst_ref=ext_ref.at[halo_at(region, size)],
            send_sem=send_sem.at[n],
            recv_sem=recv_sem.at[n],
            device_id=device_at([-d for d in region]),
            device_id_type=MESH,
        )
        copy.start()
        copies.append(copy)
    for copy in copies:
        copy.wait()


def halo_call(local):
    cx, cy, cz, rows, slots = local.shape
    vm = pl.BlockSpec(memory_space=pltpu.VMEM)
    return pl.pallas_call(
        functools.partial(halo_kernel, (cx, cy, cz)),
        out_shape=jax.ShapeDtypeStruct((cx + 1, cy + 2, cz + 2, rows, slots), jnp.float32),
        in_specs=[vm],
        out_specs=vm,
        scratch_shapes=[pltpu.SemaphoreType.DMA((len(REGIONS),))] * 2,
        compiler_params=pltpu.CompilerParams(collective_id=0, has_side_effects=True),
    )(local)


def phases():
    nx, ny, nz = sizes()
    plane = [(0, y, z) for y in range(ny) for z in range(nz)]
    if nx * ny * nz <= 16:
        return ([(x, y, z) for x in range(nx) for _, y, z in plane][1:],)
    return plane[1:], [(x, 0, 0) for x in range(1, nx)]


def return_kernel(size, part_ref, energy_ref, force_ref, total_ref, *scratch):
    sums = phases()
    buffers = scratch[: len(REGIONS)]
    arrived = scratch[len(REGIONS) : len(REGIONS) + len(sums)]
    mine, send_sem, recv_sem = scratch[len(REGIONS) + len(sums) : len(REGIONS) + len(sums) + 3]
    sum_sems = scratch[len(REGIONS) + len(sums) + 3 :]
    meet([*REGIONS, *(step for steps in sums for step in steps)])
    pending = []
    energy = energy_ref[...]

    def send_energy(p, source):
        copies = []
        for n, step in enumerate(sums[p]):
            copy = pltpu.make_async_remote_copy(
                src_ref=source,
                dst_ref=arrived[p].at[n],
                send_sem=sum_sems[2 * p].at[n],
                recv_sem=sum_sems[2 * p + 1].at[n],
                device_id=device_at(step),
                device_id_type=MESH,
            )
            copy.start()
            copies.append(copy)
        return copies

    first = send_energy(0, energy_ref)
    for n, region in enumerate(REGIONS):
        copy = pltpu.make_async_remote_copy(
            src_ref=part_ref.at[halo_at(region, size)],
            dst_ref=buffers[n],
            send_sem=send_sem.at[n],
            recv_sem=recv_sem.at[n],
            device_id=device_at(region),
            device_id_type=MESH,
        )
        copy.start()
        pending.append(copy)
    for p in range(len(sums)):
        copies = first if p == 0 else send_energy(p, mine)
        for n, copy in enumerate(copies):
            copy.wait()
            energy = energy + arrived[p][n]
        if p + 1 < len(sums):
            mine[...] = energy
    total_ref[...] = jnp.sum(energy, axis=0, keepdims=True)
    cx, cy, cz = size
    force_ref[...] = part_ref[pl.ds(0, cx), pl.ds(1, cy), pl.ds(1, cz)]
    for n, region in enumerate(REGIONS):
        pending[n].wait()
        force_ref[edge_at(region, size)] += buffers[n][...]


def return_call(part, energy, size):
    slots = part.shape[-1]
    vm = pl.BlockSpec(memory_space=pltpu.VMEM)
    sums = phases()

    def extent(region):
        return tuple(s.size for s in edge_at(region, size)) + part.shape[3:]

    return pl.pallas_call(
        functools.partial(return_kernel, size),
        out_shape=(
            jax.ShapeDtypeStruct((*size, *part.shape[3:]), jnp.float32),
            jax.ShapeDtypeStruct((1, slots), jnp.float32),
        ),
        in_specs=[vm, vm],
        out_specs=(vm, vm),
        scratch_shapes=[
            *(pltpu.VMEM(extent(region), jnp.float32) for region in REGIONS),
            *(pltpu.VMEM((len(steps), *energy.shape), jnp.float32) for steps in sums),
            pltpu.VMEM(energy.shape, jnp.float32),
            *[pltpu.SemaphoreType.DMA((len(REGIONS),))] * 2,
            *(pltpu.SemaphoreType.DMA((len(steps),)) for steps in sums for _ in range(2)),
        ],
        compiler_params=pltpu.CompilerParams(collective_id=1, has_side_effects=True),
    )(part, energy)


def on_device(coords, charges, atom_types, counts, c6_table, c12_table):
    cx, cy, cz, _, slots = coords.shape
    nt = c6_table.shape[0]
    occ = jnp.arange(slots, dtype=jnp.int32) < counts[..., None]
    charge = jnp.where(occ, charges, 0.0)
    kind = jnp.where(occ, atom_types, nt).astype(jnp.float32)
    local = jnp.concatenate(
        [coords, charge[..., None, :], kind[..., None, :], jnp.zeros((cx, cy, cz, 3, slots), jnp.float32)], axis=3
    )
    ext = halo_call(local)
    ex, ey, ez = cx + 1, cy + 2, cz + 2
    part, energy = pair_call(cx, cy, cz, nt, slots, ext.reshape(ex * ey * ez, 8, slots), c6_table, c12_table)
    forces, energy = return_call(part.reshape(ex, ey, ez, 3, slots), energy, (cx, cy, cz))
    return forces, jnp.sum(energy).reshape(1)


def solution(mesh):
    return jax.shard_map(
        on_device,
        mesh=mesh,
        in_specs=(
            P(("groups", "gx"), "gy", "gz", None, None),
            P(("groups", "gx"), "gy", "gz", None),
            P(("groups", "gx"), "gy", "gz", None),
            P(("groups", "gx"), "gy", "gz"),
            P(),
            P(),
        ),
        out_specs=(P(("groups", "gx"), "gy", "gz", None, None), P("groups")),
        check_vma=False,
    )
```

time: 120 us -> 84.3 us (0.70)
  waiting for transfers between devices: 19.6 us -> 0 us
  starting transfers between devices: 13.4 us -> 0 us
  Pallas kernels: 80.2 us -> 78.2 us
    pallas_call x1, Pallas kernels: 80.2 us -> 52.9 us  [pair_call(): pl.pallas_call(functools.partial(pair_kernel, cx, cy, cz, nt), out_shape=...]
    pallas_call x0 -> x2, Pallas kernels: none -> 25.3 us  [the longest x1 13.8 us: halo_call(): pl.pallas_call(functools.partial(halo_kernel, (cx, cy, cz)), out_shape=ja...]
    ppermute x10 -> x0, waiting for transfers between devices: 19.6 us -> none  [shifted(): return lax.ppermute(block, axis, route)]
    ppermute x10 -> x0, starting transfers between devices: 13.4 us -> none  [shifted(): return lax.ppermute(block, axis, route)]
  transfers between devices with their start and end apart: 10 -> 0, of which waited for: 8 -> 0; matrix products, arithmetic and copies ran while one was open for 1% -> 0% of each run, Pallas kernels for 0% -> 0%
where the time goes in v2:
time: 84.3 us; the launch traced here: 84 us
  Pallas kernels  78.2 us (93%)
  other arithmetic  2.91 us (3%)
  local copies, waits for them, and re-layouts  2.15 us (3%)
    pallas_call x1, Pallas kernels, pair_call(): pl.pallas_call(functools.partial(pair_kernel, cx, cy, cz, nt), out_shape=...  52.9 us
    pallas_call x1, Pallas kernels, halo_call(): pl.pallas_call(functools.partial(halo_kernel, (cx, cy, cz)), out_shape=ja...  13.8 us
    pallas_call x1, Pallas kernels, return_call(): pl.pallas_call(functools.partial(return_kernel, size), out_shape=(jax.Sha...  11.5 us
    unnamed x6, local copies, waits for them, and re-layouts  2.07 us

profile of v2, /device:TPU:0, one launch (start us, length us, event | category | flops | bytes accessed | tf_op | source)
XLA Modules:
  0.0 84.0 jit_solution(7250133642034457816)
XLA Ops:
  0.6 0.0 copy-start
  0.6 0.1 pad.3.clone
  0.7 0.8 fusion
  1.5 0.8 select_convert_fusion
  2.3 0.0 copy-done
  2.3 0.7 maximum_maximum_fusion.local_ref
  3.1 13.8 %shard_map.77 = f32[2,6,10,8,128]{4,3,2,1,0:T(8,128)} custom-call(f32[1,4,8,8,128]{4,3,2,1,0:T(8,128)} %maximum_maximum_fusion.local_ref), custom_call_target="tpu_custom_call" | custom-call | tf_op jit(solution)/shard_map/pallas_call | solution.py:363
  16.9 52.9 %shard_map.78 = (f32[120,3,128]{2,1,0:T(4,128)}, f32[8,128]{1,0:T(8,128)}) custom-call(f32[120,8,128]{2,1,0:T(8,128)} %bitcast.8, f32[64,64]{1,0:T(8,128)} %c6_ref.1, f32[64,64]{1,0:T(8,128)} %c12_ref.1), custom_call_target="tpu_custom_call" | custom-call | tf_op jit(solution)/shard_map/pallas_call | solution.py:271
  69.8 11.5 %shard_map.79 = (f32[1,4,8,3,128]{4,3,2,1,0:T(4,128)}, f32[1,128]{1,0:T(1,128)}) custom-call(f32[2,6,10,3,128]{4,3,2,1,0:T(4,128)} %bitcast.9, f32[8,128]{1,0:T(8,128)} %get-tuple-element.7.energy_ref), custom_call_target="tpu_custom_call" | custom-call | tf_op jit(solution)/shard_map/pallas_call | solution.py:441
  81.3 0.0 copy-start.1
  81.3 0.6 copy-done.1
  81.9 0.6 reduce_sum.9
  82.5 1.5 %copy.10 = f32[1,4,8,3,128]{4,2,3,1,0:T(8,128)} copy(f32[1,4,8,3,128]{4,3,2,1,0:T(4,128)} %get-tuple-element.10) | data formatting | bytes 98304
  (2 shorter events, 0.0 us)
Async XLA Ops:
  0.6 1.7 %copy-start = (f32[1,4,8,3,128]{4,2,3,1,0:T(8,128)S(1)}, f32[1,4,8,3,128]{4,2,3,1,0:T(8,128)}, u32[]{:S(2)}) copy-start(f32[1,4,8,3,128]{4,2,3,1,0:T(8,128)} %param.6) | copy-start | bytes 147460
  81.3 0.6 copy-start.1

commit v3 on v1

v3 whole, which is shorter than its diff:
```python
import functools

import jax
import jax.numpy as jnp
from jax import lax
from jax.experimental import pallas as pl
from jax.experimental.pallas import tpu as pltpu
from jax.sharding import PartitionSpec as P

CELL_EDGE = 1.1
SOFTEN = 0.09
ENERGY_UNIT = 0.1
EDGE_V = 1.0 / (1.0 + SOFTEN)
E0 = EDGE_V**0.5
E3 = EDGE_V**3
STRIP = 128
WITHIN = ((0, 1, 2), (3, 13))
BEYOND = ((4, 5, 6), (7, 8, 9), (10, 11, 12))
OFFSETS = (
    (0, 0, 1), (0, 1, -1), (0, 1, 0), (0, 1, 1),
    (1, -1, -1), (1, -1, 0), (1, -1, 1),
    (1, 0, -1), (1, 0, 0), (1, 0, 1),
    (1, 1, -1), (1, 1, 0), (1, 1, 1), (0, 0, 0),
)
AXIS_SHIFTS = ((0, 0), (0, 1), (1, -1), (1, 0), (1, 1), (2, -1), (2, 0), (2, 1))
FEATS = 32


def rounded(value):
    return value.astype(jnp.bfloat16).astype(jnp.float32)


def two_parts(value):
    high = rounded(value)
    return high, rounded(value - high)


def three_parts(value):
    high = rounded(value)
    rest = value - high
    middle = rounded(rest)
    return high, middle, rounded(rest - middle)


def pick_rows(rows, choices):
    out = jnp.zeros(rows.shape, jnp.float32)
    for r, value in enumerate(choices):
        if value is not None:
            out = jnp.where(rows == r, value, out)
    return out


def dot(a, b):
    return jnp.dot(a, b, preferred_element_type=jnp.float32)


def unroll_of(count, most):
    return max(u for u in range(1, most + 1) if count % u == 0)


def unrolled(count, most, body):
    u = unroll_of(count, most)

    def step(i, carry):
        for k in range(u):
            body(i * u + k)
        return carry

    lax.fori_loop(0, count // u, step, 0)


MESH = pl.DeviceIdType.MESH
AXES = ("gx", "gy", "gz")
REGIONS = (
    (1, 0, 0), (1, 1, 0), (1, -1, 0), (1, 0, 1), (1, 0, -1), (1, 1, 1), (1, 1, -1), (1, -1, 1), (1, -1, -1),
    (0, 1, 0), (0, 1, 1), (0, 1, -1), (0, 0, 1), (0, 0, -1),
)


def sizes():
    return tuple(lax.axis_size(name) for name in AXES)


def device_at(step):
    return {name: lax.rem(lax.axis_index(name) + d % n, n) for name, d, n in zip(AXES, step, sizes())}


def wrapped(step):
    return tuple(d % n for d, n in zip(step, sizes()))


def meet(steps):
    barrier = pltpu.get_barrier_semaphore()
    near = {wrapped(s) for s in steps} | {wrapped([-d for d in s]) for s in steps}
    near = sorted(near - {(0, 0, 0)})
    for step in near:
        pl.semaphore_signal(barrier, inc=1, device_id=device_at(step), device_id_type=MESH)
    pl.semaphore_wait(barrier, len(near))


def halo_at(region, size):
    cx, cy, cz = size
    x = pl.ds(cx, 1) if region[0] else pl.ds(0, cx)
    y = {-1: pl.ds(0, 1), 0: pl.ds(1, cy), 1: pl.ds(cy + 1, 1)}[region[1]]
    z = {-1: pl.ds(0, 1), 0: pl.ds(1, cz), 1: pl.ds(cz + 1, 1)}[region[2]]
    return x, y, z


def edge_at(region, size):
    cx, cy, cz = size
    x = pl.ds(0, 1) if region[0] else pl.ds(0, cx)
    y = {-1: pl.ds(cy - 1, 1), 0: pl.ds(0, cy), 1: pl.ds(0, 1)}[region[1]]
    z = {-1: pl.ds(cz - 1, 1), 0: pl.ds(0, cz), 1: pl.ds(0, 1)}[region[2]]
    return x, y, z


def phases():
    nx, ny, nz = sizes()
    plane = [(0, y, z) for y in range(ny) for z in range(nz)]
    if nx * ny * nz <= 16:
        return ([(x, y, z) for x in range(nx) for _, y, z in plane][1:],)
    return plane[1:], [(x, 0, 0) for x in range(1, nx)]


def pair_kernel(size, nt, coords_ref, charge_ref, type_ref, count_ref, c6_ref, c12_ref, force_ref, energy_ref,
                local, ext, part, lh, lc, pos, wc, blocks, xi, gg, fb, fa, esum, *scratch):
    cx, cy, cz = size
    ey = cy + 2
    ez = cz + 2
    slots = 128
    n_ext = (cx + 1) * ey * ez
    n_own = cx * cy * cz
    bf = jnp.bfloat16
    buffers = scratch[: len(REGIONS)]
    send_sem, recv_sem, back_send, back_recv = scratch[len(REGIONS) : len(REGIONS) + 4]
    sums = phases()
    arrived = scratch[len(REGIONS) + 4 : len(REGIONS) + 4 + len(sums)]
    sum_sems = scratch[len(REGIONS) + 4 + len(sums) :]
    rows = lax.broadcasted_iota(jnp.int32, (8, slots), 0)
    lanes = lax.broadcasted_iota(jnp.int32, (1, slots), 1)
    ids = lax.broadcasted_iota(jnp.int32, (nt, slots), 0).astype(jnp.float32)
    one = jnp.ones((1, slots), jnp.float32)

    for x in range(cx):
        for y in range(cy):
            for z in range(cz):
                occupied = lanes < count_ref[x, y, z]
                charge = jnp.where(occupied, charge_ref[x, y, z : z + 1, :], 0.0)
                kind = jnp.where(occupied, type_ref[x, y, z : z + 1, :], nt).astype(jnp.float32)
                tile = jnp.concatenate([coords_ref[x, y, z], charge, kind, jnp.zeros((3, slots), jnp.float32)], axis=0)
                local[x, y, z] = tile
                ext[x, y + 1, z + 1] = tile

    meet([*REGIONS, *(step for steps in sums for step in steps)])
    copies = {}
    for n, region in enumerate(REGIONS):
        copies[region] = pltpu.make_async_remote_copy(
            src_ref=local.at[edge_at(region, size)],
            dst_ref=ext.at[halo_at(region, size)],
            send_sem=send_sem.at[n],
            recv_sem=recv_sem.at[n],
            device_id=device_at([-d for d in region]),
            device_id_type=MESH,
        )
    for plane in (0, 1):
        for region in REGIONS:
            if region[0] == plane:
                copies[region].start()

    c6 = c6_ref[...]
    c12 = c12_ref[...]
    c12 = (0.5 * ENERGY_UNIT) * (c12 + c12.T)
    c6 = (0.5 * ENERGY_UNIT) * (c6 + c6.T) - (2.0 * E3) * c12
    both = jnp.concatenate([c12, c6], axis=0)
    high = both.astype(bf)
    low = (both - high.astype(jnp.float32)).astype(bf)

    def flat(p):
        return (p[0] * ey + p[1]) * ez + p[2]

    def place(a):
        return a // (cy * cz), (a // cz) % cy + 1, a % cz + 1

    def prepare(p):
        c = flat(p)
        f = ext[p[0], p[1], p[2]]
        hot = (ids == f[4:5, :]).astype(jnp.float32).astype(bf)
        parts = [two_parts(f[k : k + 1, :] - 0.5 * CELL_EDGE) for k in range(3)]
        feats = []
        norm = None
        for h, m in parts:
            feats.append(pick_rows(rows, (h, h, m, m, one, one, one)))
            x = h + m
            norm = x * x if norm is None else norm + x * x
        qh, qm = two_parts(f[3:4, :])
        feats.append(pick_rows(rows, (*three_parts(norm), qh, qh, qm, qm)))
        (xh, xm), (yh, ym), (zh, zm) = parts
        pos[c] = pick_rows(rows, (xh, xm, yh, ym, zh, zm, one))
        lc[c] = jnp.concatenate(feats, axis=0).astype(bf).T
        lh[c] = jnp.concatenate([hot, hot], axis=0).T
        fb[c] = jnp.zeros((slots, slots), jnp.float32)

    def weights(a):
        x, y, z = place(a)
        f = ext[x, y, z]
        hot = (ids == f[4:5, :]).astype(jnp.float32).astype(bf)
        th = dot(high, hot).astype(bf)
        tl = dot(low, hot).astype(bf)
        wc[a, :, :slots] = jnp.concatenate([th[:nt], tl[:nt]], axis=0)
        wc[a, :, slots:] = jnp.concatenate([th[nt:], tl[nt:]], axis=0)
        for n, (k, shift) in enumerate(AXIS_SHIFTS):
            h, m = two_parts(f[k : k + 1, :] - (0.5 * CELL_EDGE + shift * CELL_EDGE))
            r = h + m
            sq = r * r
            if k == 0:
                sq = sq + SOFTEN
            h2 = -2.0 * h
            m2 = -2.0 * m
            blocks[a, n] = pick_rows(rows, (h2, m2, h2, m2, *three_parts(sq)))
        qh, qm = two_parts(ENERGY_UNIT * f[3:4, :])
        blocks[a, len(AXIS_SHIFTS)] = pick_rows(rows, (None, None, None, qh, qm, qh, qm))
        group = pos[flat((x, y, z))]
        xt = jnp.concatenate([group] * (slots // 8), axis=0).astype(bf).T
        xi[a] = jnp.concatenate([xt, xt], axis=0)

    norm_block = jnp.where(rows < 3, 1.0, 0.0)
    zero_block = jnp.zeros((8, slots), jnp.float32)
    strip_rows = lax.broadcasted_iota(jnp.int32, (STRIP, slots), 0)
    strip_lanes = lax.broadcasted_iota(jnp.int32, (STRIP, slots), 1)

    def neighbour(a, n):
        o = OFFSETS[n]
        return flat(place(a)) + (o[0] * ey + o[1]) * ez + o[2]

    def forward(a, members):
        v1 = dot(jnp.concatenate([lh[neighbour(a, n)] for n in members], axis=0), wc[a])
        v2 = []
        charge = jnp.concatenate([zero_block] * 3 + [blocks[a, len(AXIS_SHIFTS)]], axis=0).astype(bf)
        for n in members:
            picks = [AXIS_SHIFTS.index((k, OFFSETS[n][k])) for k in range(3)]
            near = jnp.concatenate([blocks[a, p] for p in picks] + [norm_block], axis=0).astype(bf)
            v2.append(dot(lc[neighbour(a, n)], jnp.concatenate([near, charge], axis=1)))
        return v1, v2

    def compute(i, members, e_acc, vals):
        v1, v2 = vals
        for j, n in enumerate(members):
            own = OFFSETS[n] == (0, 0, 0)
            for r in range(0, slots, STRIP):
                at = pl.ds(j * slots + r, STRIP)
                t = v2[j][r : r + STRIP, :slots]
                charge = v2[j][r : r + STRIP, slots:]
                c12p = v1[j * slots + r : j * slots + r + STRIP, :slots]
                c6p = v1[j * slots + r : j * slots + r + STRIP, slots:]
                s = lax.rsqrt(t)
                v = s * s
                z3 = v * v * v
                w = jnp.maximum((1.0 + SOFTEN) - t, 0.0)
                if own:
                    w = jnp.where(strip_rows + r == strip_lanes, 0.0, w)
                y = z3 - E3
                m = c12p * y
                b1 = m - c6p
                u = y * b1 + charge * (s - E0)
                h = (z3 * (b1 + m)) * 6.0 + charge * s
                uw = u * w
                e = jnp.sum((uw * w).reshape(STRIP // 8, 8, slots), axis=0)
                e_acc = e_acc + (0.5 * e if own else e)
                g = w * (v * w * h) + 4.0 * uw
                gh = g.astype(bf)
                gg[i, at, :slots] = gh
                gg[i, at, slots:] = (g - gh.astype(jnp.float32)).astype(bf)
        return e_acc

    def spread(a, i, members):
        out = dot(gg[i, pl.ds(0, slots * len(members)), :], xi[a])
        for j, n in enumerate(members):
            b = neighbour(a, n)
            if OFFSETS[n] != (0, 0, 0):
                fb[b, :, 8 * n : 8 * n + 8] = out[j * slots : (j + 1) * slots, 8 * n : 8 * n + 8]
            got = dot(pos[b].astype(bf), gg[i, pl.ds(j * slots, slots), :])
            fa[n] = got[:, :slots] + got[:, slots:]

    def shift_sum(parts):
        total = None
        extra = [zero_block] * 3
        for n, value in parts:
            total = value if total is None else total + value
            for k in range(3):
                o = OFFSETS[n][k]
                if o:
                    extra[k] = extra[k] + value if o > 0 else extra[k] - value
        return total, extra

    def force_of(c, parts, sign):
        total, extra = shift_sum(parts)
        x = pos[c]
        s = total[6:7]
        out = []
        for k in range(3):
            here = x[2 * k : 2 * k + 1] + x[2 * k + 1 : 2 * k + 2]
            moved = total[2 * k : 2 * k + 1] + total[2 * k + 1 : 2 * k + 2] + (sign * CELL_EDGE) * extra[k][6:7]
            out.append(here * s - moved)
        return jnp.concatenate(out, axis=0)

    def run(low_a, high_a, groups, e_acc):
        span = high_a - low_a
        names = [n for members in groups for n in members]
        last = len(groups) - 1
        gg[last] = jnp.zeros(gg.shape[1:], bf)
        fa[...] = jnp.zeros(fa.shape, jnp.float32)

        def finish(a):
            x, y, z = place(a)
            part[x, y, z] += force_of(flat((x, y, z)), [(n, fa[n]) for n in names], 1.0)

        def cell(a, e_acc):
            before = low_a + (a - low_a + span - 1) % span
            vals = forward(a, groups[0])
            for i, members in enumerate(groups):
                ahead = forward(a, groups[i + 1]) if i < last else None
                e_acc = compute(i, members, e_acc, vals)
                vals = ahead
                if i:
                    spread(a, i - 1, groups[i - 1])
                else:
                    spread(before, last, groups[last])
                    finish(before)
            return e_acc

        e_acc = lax.fori_loop(low_a, high_a, cell, e_acc)
        spread(high_a - 1, last, groups[last])
        finish(high_a - 1)
        return e_acc

    def gathered(c):
        turned = fb[c].T
        return force_of(c, [(n, turned[8 * n : 8 * n + 8]) for n in range(len(OFFSETS) - 1)], -1.0)

    def gather(p):
        part[p[0], p[1], p[2]] = gathered(flat(p))

    def top_row(body):
        unrolled(cx * ez, 5, lambda i: body((i // ez, cy + 1, i % ez)))

    def side_columns(body):
        unrolled(2 * cx * cy, 4, lambda i: body((i // (2 * cy), (i // 2) % cy + 1, (i % 2) * (cz + 1))))

    def far_plane(body):
        unrolled(ey * ez, 5, lambda i: body((cx, i // ez, i % ez)))

    def send_back(plane):
        for n, region in enumerate(REGIONS):
            if region[0] == plane:
                back[region] = pltpu.make_async_remote_copy(
                    src_ref=part.at[halo_at(region, size)],
                    dst_ref=buffers[n],
                    send_sem=back_send.at[n],
                    recv_sem=back_recv.at[n],
                    device_id=device_at(region),
                    device_id_type=MESH,
                )
                back[region].start()

    def send_energy(p):
        started = []
        for n, step in enumerate(sums[p]):
            copy = pltpu.make_async_remote_copy(
                src_ref=esum.at[p],
                dst_ref=arrived[p].at[n],
                send_sem=sum_sems[2 * p].at[n],
                recv_sem=sum_sems[2 * p + 1].at[n],
                device_id=device_at(step),
                device_id_type=MESH,
            )
            copy.start()
            started.append(copy)
        return started

    back = {}
    unrolled(n_own, 4, lambda a: prepare(place(a)))
    unrolled(n_own, 4, weights)
    part[...] = jnp.zeros(part.shape, jnp.float32)
    for region in REGIONS:
        if region[0] == 0:
            copies[region].wait()
    top_row(prepare)
    side_columns(prepare)
    half = n_own // 2
    e = run(0, half, WITHIN, zero_block)
    for region in REGIONS:
        if region[0] == 1:
            copies[region].wait()
    far_plane(prepare)
    e = run(0, n_own, BEYOND, e)
    far_plane(gather)
    send_back(1)
    e = run(half, n_own, WITHIN, e)
    esum[0] = e
    top_row(gather)
    side_columns(gather)
    started = send_energy(0)
    send_back(0)

    def own_force(a):
        x, y, z = place(a)
        force_ref[x, y - 1, z - 1] = part[x, y, z] + gathered(flat((x, y, z)))

    unrolled(n_own, 4, own_force)
    for plane in (1, 0):
        for n, region in enumerate(REGIONS):
            if region[0] == plane:
                back[region].wait()
                force_ref[edge_at(region, size)] += buffers[n][...]
    for p in range(len(sums)):
        for n, copy in enumerate(started):
            copy.wait()
            e = e + arrived[p][n]
        if p + 1 < len(sums):
            esum[p + 1] = e
            started = send_energy(p + 1)
    energy_ref[0, 0] = jnp.sum(e)


def on_device(coords, charges, atom_types, counts, c6_table, c12_table):
    cx, cy, cz, _, slots = coords.shape
    nt = c6_table.shape[0]
    size = (cx, cy, cz)
    n_ext = (cx + 1) * (cy + 2) * (cz + 2)
    n = cx * cy * cz
    f32 = jnp.float32
    bf = jnp.bfloat16
    vm = pl.BlockSpec(memory_space=pltpu.VMEM)
    sm = pl.BlockSpec(memory_space=pltpu.SMEM)
    grid = (cx + 1, cy + 2, cz + 2)
    sums = phases()
    most = max(len(members) for members in WITHIN + BEYOND)

    def extent(region):
        return tuple(s.size for s in edge_at(region, size)) + (3, slots)

    forces, energy = pl.pallas_call(
        functools.partial(pair_kernel, size, nt),
        out_shape=(
            jax.ShapeDtypeStruct(coords.shape, f32),
            jax.ShapeDtypeStruct((1, 1), f32),
        ),
        in_specs=[vm, vm, vm, sm, vm, vm],
        out_specs=(vm, sm),
        scratch_shapes=[
            pltpu.VMEM((*size, 8, slots), f32),
            pltpu.VMEM((*grid, 8, slots), f32),
            pltpu.VMEM((*grid, 3, slots), f32),
            pltpu.VMEM((n_ext, slots, slots), bf),
            pltpu.VMEM((n_ext, slots, FEATS), bf),
            pltpu.VMEM((n_ext, 8, slots), f32),
            pltpu.VMEM((n, slots, 2 * slots), bf),
            pltpu.VMEM((n, len(AXIS_SHIFTS) + 1, 8, slots), f32),
            pltpu.VMEM((n, 2 * slots, slots), bf),
            pltpu.VMEM((max(len(WITHIN), len(BEYOND)), most * slots, 2 * slots), bf),
            pltpu.VMEM((n_ext, slots, slots), f32),
            pltpu.VMEM((len(OFFSETS), 8, slots), f32),
            pltpu.VMEM((len(sums), 8, slots), f32),
            *(pltpu.VMEM(extent(region), f32) for region in REGIONS),
            *[pltpu.SemaphoreType.DMA((len(REGIONS),))] * 4,
            *(pltpu.VMEM((len(steps), 8, slots), f32) for steps in sums),
            *(pltpu.SemaphoreType.DMA((len(steps),)) for steps in sums for _ in range(2)),
        ],
        compiler_params=pltpu.CompilerParams(
            collective_id=0, has_side_effects=True, vmem_limit_bytes=56 * 2**20
        ),
    )(coords, charges, atom_types, counts, c6_table, c12_table)
    return forces, energy.reshape(1)


def solution(mesh):
    return jax.shard_map(
        on_device,
        mesh=mesh,
        in_specs=(
            P(("groups", "gx"), "gy", "gz", None, None),
            P(("groups", "gx"), "gy", "gz", None),
            P(("groups", "gx"), "gy", "gz", None),
            P(("groups", "gx"), "gy", "gz"),
            P(),
            P(),
        ),
        out_specs=(P(("groups", "gx"), "gy", "gz", None, None), P("groups")),
        check_vma=False,
    )
```

time: 120 us -> 75 us (0.62)
  waiting for transfers between devices: 19.6 us -> 0 us
  starting transfers between devices: 13.4 us -> 0 us
  Pallas kernels: 80.2 us -> 69.3 us
  other arithmetic: 2.62 us -> 0 us
  between operations: 0.88 us -> 2.45 us
    ppermute x10 -> x0, waiting for transfers between devices: 19.6 us -> none  [shifted(): return lax.ppermute(block, axis, route)]
    ppermute x10 -> x0, starting transfers between devices: 13.4 us -> none  [shifted(): return lax.ppermute(block, axis, route)]
    pallas_call x1, Pallas kernels: 80.2 us -> 69.3 us  [on_device(): pl.pallas_call(functools.partial(pair_kernel, size, nt), out_shape=(jax.S...]
    unnamed x10 -> x2, local copies, waits for them, and re-layouts: 1.39 us -> 2.9 us
    reduce_sum x2 -> x0, other arithmetic: 1.34 us -> none  [the longest x1 0.74 us: on_device(): energy = jnp.sum(energy, axis=0, keepdims=True)]
  transfers between devices with their start and end apart: 10 -> 0, of which waited for: 8 -> 0; matrix products, arithmetic and copies ran while one was open for 1% -> 0% of each run, Pallas kernels for 0% -> 0%
where the time goes in v3:
time: 75 us; the launch traced here: 74.7 us
  Pallas kernels  69.3 us (92%)
  local copies, waits for them, and re-layouts  2.9 us (4%)
  between operations  2.45 us (3%)
    pallas_call x1, Pallas kernels, on_device(): pl.pallas_call(functools.partial(pair_kernel, size, nt), out_shape=(jax.S...  69.3 us
    unnamed x2, local copies, waits for them, and re-layouts  2.9 us

profile of v3, /device:TPU:0, one launch (start us, length us, event | category | flops | bytes accessed | tf_op | source)
XLA Modules:
  0.0 74.7 jit_solution(4993231318565604784)
XLA Ops:
  0.6 1.4 %copy.8.coords_ref = f32[1,4,8,3,128]{4,3,2,1,0:T(4,128)} copy(f32[1,4,8,3,128]{4,2,3,1,0:T(8,128)} %param.6) | data formatting | bytes 98304 | tf_op args[0]
  2.1 69.3 %shard_map.77 = (f32[1,4,8,3,128]{4,3,2,1,0:T(4,128)}, f32[1,1]{1,0:T(1,128)}) custom-call(f32[1,4,8,3,128]{4,3,2,1,0:T(4,128)} %copy.8.coords_ref, f32[1,4,8,128]{3,2,1,0:T(8,128)} %charge_ref.1, s32[1,4,8,128]{3,2,1,0:T(8,128)} %type_ref.1, s32[1,4,8]{2,1,0:T(4,128)} %count_ref.1, f32[64,64]{1,0:T(8,128)} %c6_ref.1, f32[64,64]{1,0:T(8,128)} %c12_ref.1), custom_call_target="tpu_custom_call" | custom-call | tf_op jit(solution)/shard_map/pallas_call | solution.py:442
  71.4 1.5 %copy.9 = f32[1,4,8,3,128]{4,2,3,1,0:T(8,128)} copy(f32[1,4,8,3,128]{4,3,2,1,0:T(4,128)} %get-tuple-element.6) | data formatting | bytes 98304

commit v4 on v3

--- a/solution.py
+++ b/solution.py
@@ -13,9 +13,10 @@
 EDGE_V = 1.0 / (1.0 + SOFTEN)
 E0 = EDGE_V**0.5
 E3 = EDGE_V**3
-STRIP = 128
+STRIP = 32
+TOGETHER = 4
 WITHIN = ((0, 1, 2), (3, 13))
-BEYOND = ((4, 5, 6), (7, 8, 9), (10, 11, 12))
+BEYOND = ((4, 5), (6, 7), (8, 9), (10, 11, 12))
 OFFSETS = (
     (0, 0, 1), (0, 1, -1), (0, 1, 0), (0, 1, 1),
     (1, -1, -1), (1, -1, 0), (1, -1, 1),
@@ -89,13 +90,13 @@
     return tuple(d % n for d, n in zip(step, sizes()))
 
 
-def meet(steps):
+def greet(steps):
     barrier = pltpu.get_barrier_semaphore()
     near = {wrapped(s) for s in steps} | {wrapped([-d for d in s]) for s in steps}
     near = sorted(near - {(0, 0, 0)})
     for step in near:
         pl.semaphore_signal(barrier, inc=1, device_id=device_at(step), device_id_type=MESH)
-    pl.semaphore_wait(barrier, len(near))
+    return len(near)
 
 
 def halo_at(region, size):
@@ -141,17 +142,17 @@
     ids = lax.broadcasted_iota(jnp.int32, (nt, slots), 0).astype(jnp.float32)
     one = jnp.ones((1, slots), jnp.float32)
 
+    greeted = greet([*REGIONS, *(step for steps in sums for step in steps)])
     for x in range(cx):
         for y in range(cy):
             for z in range(cz):
                 occupied = lanes < count_ref[x, y, z]
                 charge = jnp.where(occupied, charge_ref[x, y, z : z + 1, :], 0.0)
                 kind = jnp.where(occupied, type_ref[x, y, z : z + 1, :], nt).astype(jnp.float32)
-                tile = jnp.concatenate([coords_ref[x, y, z], charge, kind, jnp.zeros((3, slots), jnp.float32)], axis=0)
+                tile = jnp.concatenate([*(coords_ref[x, y, k, z : z + 1, :] for k in range(3)), charge, kind, jnp.zeros((3, slots), jnp.float32)], axis=0)
                 local[x, y, z] = tile
                 ext[x, y + 1, z + 1] = tile
 
-    meet([*REGIONS, *(step for steps in sums for step in steps)])
     copies = {}
     for n, region in enumerate(REGIONS):
         copies[region] = pltpu.make_async_remote_copy(
@@ -162,11 +163,6 @@
             device_id=device_at([-d for d in region]),
             device_id_type=MESH,
         )
-    for plane in (0, 1):
-        for region in REGIONS:
-            if region[0] == plane:
-                copies[region].start()
-
     c6 = c6_ref[...]
     c12 = c12_ref[...]
     c12 = (0.5 * ENERGY_UNIT) * (c12 + c12.T)
@@ -228,18 +224,22 @@
     strip_rows = lax.broadcasted_iota(jnp.int32, (STRIP, slots), 0)
     strip_lanes = lax.broadcasted_iota(jnp.int32, (STRIP, slots), 1)
 
-    def neighbour(a, n):
+    def own_index(p):
+        return (p[0] * cy + p[1] - 1) * cz + p[2] - 1
+
+    def neighbour(p, n):
         o = OFFSETS[n]
-        return flat(place(a)) + (o[0] * ey + o[1]) * ez + o[2]
-
-    def forward(a, members):
-        v1 = dot(jnp.concatenate([lh[neighbour(a, n)] for n in members], axis=0), wc[a])
+        return flat(p) + (o[0] * ey + o[1]) * ez + o[2]
+
+    def forward(p, members):
+        a = own_index(p)
+        v1 = dot(jnp.concatenate([lh[neighbour(p, n)] for n in members], axis=0), wc[a])
         v2 = []
         charge = jnp.concatenate([zero_block] * 3 + [blocks[a, len(AXIS_SHIFTS)]], axis=0).astype(bf)
         for n in members:
             picks = [AXIS_SHIFTS.index((k, OFFSETS[n][k])) for k in range(3)]
-            near = jnp.concatenate([blocks[a, p] for p in picks] + [norm_block], axis=0).astype(bf)
-            v2.append(dot(lc[neighbour(a, n)], jnp.concatenate([near, charge], axis=1)))
+            near = jnp.concatenate([blocks[a, k] for k in picks] + [norm_block], axis=0).astype(bf)
+            v2.append(dot(lc[neighbour(p, n)], jnp.concatenate([near, charge], axis=1)))
         return v1, v2
 
     def compute(i, members, e_acc, vals):
@@ -272,14 +272,14 @@
                 gg[i, at, slots:] = (g - gh.astype(jnp.float32)).astype(bf)
         return e_acc
 
-    def spread(a, i, members):
-        out = dot(gg[i, pl.ds(0, slots * len(members)), :], xi[a])
+    def spread(p, k, i, members):
+        out = dot(gg[i, pl.ds(0, slots * len(members)), :], xi[own_index(p)])
         for j, n in enumerate(members):
-            b = neighbour(a, n)
+            b = neighbour(p, n)
             if OFFSETS[n] != (0, 0, 0):
                 fb[b, :, 8 * n : 8 * n + 8] = out[j * slots : (j + 1) * slots, 8 * n : 8 * n + 8]
             got = dot(pos[b].astype(bf), gg[i, pl.ds(j * slots, slots), :])
-            fa[n] = got[:, :slots] + got[:, slots:]
+            fa[k, n] = got[:, :slots] + got[:, slots:]
 
     def shift_sum(parts):
         total = None
@@ -303,35 +303,52 @@
             out.append(here * s - moved)
         return jnp.concatenate(out, axis=0)
 
-    def run(low_a, high_a, groups, e_acc):
-        span = high_a - low_a
+    def run(count, place_of, groups, e_acc):
+        if not count:
+            return e_acc
         names = [n for members in groups for n in members]
-        last = len(groups) - 1
+        cells = unroll_of(count, TOGETHER)
+        plan = [(k, members) for k in range(cells) for members in groups]
+        last = len(plan) - 1
         gg[last] = jnp.zeros(gg.shape[1:], bf)
         fa[...] = jnp.zeros(fa.shape, jnp.float32)
 
-        def finish(a):
-            x, y, z = place(a)
-            part[x, y, z] += force_of(flat((x, y, z)), [(n, fa[n]) for n in names], 1.0)
-
-        def cell(a, e_acc):
-            before = low_a + (a - low_a + span - 1) % span
-            vals = forward(a, groups[0])
-            for i, members in enumerate(groups):
-                ahead = forward(a, groups[i + 1]) if i < last else None
-                e_acc = compute(i, members, e_acc, vals)
+        def finish(p, k):
+            part[p[0], p[1], p[2]] += force_of(flat(p), [(n, fa[k, n]) for n in names], 1.0)
+
+        def cell(i, e_acc):
+            places = [place_of(i * cells + k) for k in range(cells)]
+            before = place_of((i * cells + count - 1) % count)
+            vals = forward(places[0], groups[0])
+            for m, (k, members) in enumerate(plan):
+                ahead = forward(places[plan[m + 1][0]], plan[m + 1][1]) if m < last else None
+                e_acc = compute(m, members, e_acc, vals)
                 vals = ahead
-                if i:
-                    spread(a, i - 1, groups[i - 1])
+                if m:
+                    done, named = plan[m - 1]
+                    spread(places[done], done, m - 1, named)
+                    if done != k:
+                        finish(places[done], done)
                 else:
-                    spread(before, last, groups[last])
-                    finish(before)
+                    spread(before, cells - 1, last, groups[-1])
+                    finish(before, cells - 1)
             return e_acc
 
-        e_acc = lax.fori_loop(low_a, high_a, cell, e_acc)
-        spread(high_a - 1, last, groups[last])
-        finish(high_a - 1)
+        e_acc = lax.fori_loop(0, count // cells, cell, e_acc)
+        spread(place_of(count - 1), cells - 1, last, groups[-1])
+        finish(place_of(count - 1), cells - 1)
         return e_acc
+
+    inner = (cy - 1) * (cz - 2)
+
+    def inside(i):
+        return i // inner, (i % inner) // (cz - 2) + 1, i % (cz - 2) + 2
+
+    def at_sides(i):
+        return i // (2 * (cy - 1)), (i // 2) % (cy - 1) + 1, (i % 2) * (cz - 1) + 1
+
+    def at_top(i):
+        return i // cz, cy, i % cz + 1
 
     def gathered(c):
         turned = fb[c].T
@@ -381,37 +398,42 @@
     unrolled(n_own, 4, lambda a: prepare(place(a)))
     unrolled(n_own, 4, weights)
     part[...] = jnp.zeros(part.shape, jnp.float32)
+    early = cx * inner // 3
+    e = run(early, inside, WITHIN, zero_block)
+    pl.semaphore_wait(pltpu.get_barrier_semaphore(), greeted)
     for region in REGIONS:
-        if region[0] == 0:
-            copies[region].wait()
+        copies[region].start()
+    e = run(cx * inner - early, lambda i: inside(i + early), WITHIN, e)
+    for region in REGIONS:
+        copies[region].wait()
     top_row(prepare)
     side_columns(prepare)
-    half = n_own // 2
-    e = run(0, half, WITHIN, zero_block)
-    for region in REGIONS:
-        if region[0] == 1:
-            copies[region].wait()
     far_plane(prepare)
-    e = run(0, n_own, BEYOND, e)
+    e = run(n_own, place, BEYOND, e)
     far_plane(gather)
     send_back(1)
-    e = run(half, n_own, WITHIN, e)
+    e = run(2 * cx * (cy - 1), at_sides, WITHIN, e)
+    e = run(cx * cz, at_top, WITHIN, e)
     esum[0] = e
     top_row(gather)
+    started = send_energy(0)
     side_columns(gather)
-    started = send_energy(0)
     send_back(0)
 
     def own_force(a):
         x, y, z = place(a)
-        force_ref[x, y - 1, z - 1] = part[x, y, z] + gathered(flat((x, y, z)))
+        total = part[x, y, z] + gathered(flat((x, y, z)))
+        for k in range(3):
+            force_ref[x, y - 1, k, pl.ds(z - 1, 1), :] = total[k : k + 1]
 
     unrolled(n_own, 4, own_force)
     for plane in (1, 0):
         for n, region in enumerate(REGIONS):
             if region[0] == plane:
                 back[region].wait()
-                force_ref[edge_at(region, size)] += buffers[n][...]
+                x, y, z = edge_at(region, size)
+                for k in range(3):
+                    force_ref[x, y, k, z, :] += buffers[n][:, :, :, k, :]
     for p in range(len(sums)):
         for n, copy in enumerate(started):
             copy.wait()
@@ -442,7 +464,7 @@
     forces, energy = pl.pallas_call(
         functools.partial(pair_kernel, size, nt),
         out_shape=(
-            jax.ShapeDtypeStruct(coords.shape, f32),
+            jax.ShapeDtypeStruct((cx, cy, 3, cz, slots), f32),
             jax.ShapeDtypeStruct((1, 1), f32),
         ),
         in_specs=[vm, vm, vm, sm, vm, vm],
@@ -457,9 +479,9 @@
             pltpu.VMEM((n, slots, 2 * slots), bf),
             pltpu.VMEM((n, len(AXIS_SHIFTS) + 1, 8, slots), f32),
             pltpu.VMEM((n, 2 * slots, slots), bf),
-            pltpu.VMEM((max(len(WITHIN), len(BEYOND)), most * slots, 2 * slots), bf),
+            pltpu.VMEM((TOGETHER * max(len(WITHIN), len(BEYOND)), most * slots, 2 * slots), bf),
             pltpu.VMEM((n_ext, slots, slots), f32),
-            pltpu.VMEM((len(OFFSETS), 8, slots), f32),
+            pltpu.VMEM((TOGETHER, len(OFFSETS), 8, slots), f32),
             pltpu.VMEM((len(sums), 8, slots), f32),
             *(pltpu.VMEM(extent(region), f32) for region in REGIONS),
             *[pltpu.SemaphoreType.DMA((len(REGIONS),))] * 4,
@@ -469,8 +491,8 @@
         compiler_params=pltpu.CompilerParams(
             collective_id=0, has_side_effects=True, vmem_limit_bytes=56 * 2**20
         ),
-    )(coords, charges, atom_types, counts, c6_table, c12_table)
-    return forces, energy.reshape(1)
+    )(jnp.swapaxes(coords, 2, 3), charges, atom_types, counts, c6_table, c12_table)
+    return jnp.swapaxes(forces, 2, 3), energy.reshape(1)
 
 
 def solution(mesh):

time: 75 us -> 62.3 us (0.83)
  Pallas kernels: 69.3 us -> 58.3 us
  local copies, waits for them, and re-layouts: 2.9 us -> 1.42 us
    pallas_call x1, Pallas kernels: 69.3 us -> 58.3 us  [on_device(): pl.pallas_call(functools.partial(pair_kernel, size, nt), out_shape=(jax.S...]
    unnamed x2 -> x1, local copies, waits for them, and re-layouts: 2.9 us -> 1.42 us
where the time goes in v4:
time: 62.3 us; the launch traced here: 62.1 us
  Pallas kernels  58.3 us (94%)
  between operations  2.38 us (4%)
  local copies, waits for them, and re-layouts  1.42 us (2%)
    pallas_call x1, Pallas kernels, on_device(): pl.pallas_call(functools.partial(pair_kernel, size, nt), out_shape=(jax.S...  58.3 us
    unnamed x1, local copies, waits for them, and re-layouts  1.42 us

profile of v4, /device:TPU:0, one launch (start us, length us, event | category | flops | bytes accessed | tf_op | source)
XLA Modules:
  0.0 62.1 jit_solution(5363348660425194329)
XLA Ops:
  0.6 58.3 %shard_map.77 = (f32[1,4,3,8,128]{4,3,2,1,0:T(8,128)}, f32[1,1]{1,0:T(1,128)}) custom-call(f32[1,4,3,8,128]{4,3,2,1,0:T(8,128)} %bitcast.4, f32[1,4,8,128]{3,2,1,0:T(8,128)} %charge_ref.1, s32[1,4,8,128]{3,2,1,0:T(8,128)} %type_ref.1, s32[1,4,8]{2,1,0:T(4,128)} %count_ref.1, f32[64,64]{1,0:T(8,128)} %c6_ref.1, f32[64,64]{1,0:T(8,128)} %c12_ref.1), custom_call_target="tpu_custom_call" | custom-call | tf_op jit(solution)/shard_map/pallas_call | solution.py:464
  58.9 1.4 %copy.10 = f32[1,4,8,3,128]{4,2,3,1,0:T(8,128)} copy(f32[1,4,8,3,128]{4,2,3,1,0:T(8,128)} %bitcast.3) | data formatting | bytes 98304

commit v5 on v4

--- a/solution.py
+++ b/solution.py
@@ -13,7 +13,7 @@
 EDGE_V = 1.0 / (1.0 + SOFTEN)
 E0 = EDGE_V**0.5
 E3 = EDGE_V**3
-STRIP = 32
+STRIP = 128
 TOGETHER = 4
 WITHIN = ((0, 1, 2), (3, 13))
 BEYOND = ((4, 5), (6, 7), (8, 9), (10, 11, 12))
@@ -358,13 +358,13 @@
         part[p[0], p[1], p[2]] = gathered(flat(p))
 
     def top_row(body):
-        unrolled(cx * ez, 5, lambda i: body((i // ez, cy + 1, i % ez)))
+        unrolled(cx * ez, 10, lambda i: body((i // ez, cy + 1, i % ez)))
 
     def side_columns(body):
-        unrolled(2 * cx * cy, 4, lambda i: body((i // (2 * cy), (i // 2) % cy + 1, (i % 2) * (cz + 1))))
+        unrolled(2 * cx * cy, 8, lambda i: body((i // (2 * cy), (i // 2) % cy + 1, (i % 2) * (cz + 1))))
 
     def far_plane(body):
-        unrolled(ey * ez, 5, lambda i: body((cx, i // ez, i % ez)))
+        unrolled(ey * ez, 10, lambda i: body((cx, i // ez, i % ez)))
 
     def send_back(plane):
         for n, region in enumerate(REGIONS):
@@ -395,7 +395,7 @@
         return started
 
     back = {}
-    unrolled(n_own, 4, lambda a: prepare(place(a)))
+    unrolled(n_own, 8, lambda a: prepare(place(a)))
     unrolled(n_own, 4, weights)
     part[...] = jnp.zeros(part.shape, jnp.float32)
     early = cx * inner // 3
@@ -424,16 +424,16 @@
         x, y, z = place(a)
         total = part[x, y, z] + gathered(flat((x, y, z)))
         for k in range(3):
-            force_ref[x, y - 1, k, pl.ds(z - 1, 1), :] = total[k : k + 1]
-
-    unrolled(n_own, 4, own_force)
+            force_ref[x, y - 1, k, pl.ds(z - 1, 1), :] = -total[k : k + 1]
+
+    unrolled(n_own, 8, own_force)
     for plane in (1, 0):
         for n, region in enumerate(REGIONS):
             if region[0] == plane:
                 back[region].wait()
                 x, y, z = edge_at(region, size)
                 for k in range(3):
-                    force_ref[x, y, k, z, :] += buffers[n][:, :, :, k, :]
+                    force_ref[x, y, k, z, :] -= buffers[n][:, :, :, k, :]
     for p in range(len(sums)):
         for n, copy in enumerate(started):
             copy.wait()
@@ -492,7 +492,7 @@
             collective_id=0, has_side_effects=True, vmem_limit_bytes=56 * 2**20
         ),
     )(jnp.swapaxes(coords, 2, 3), charges, atom_types, counts, c6_table, c12_table)
-    return jnp.swapaxes(forces, 2, 3), energy.reshape(1)
+    return -jnp.swapaxes(forces, 2, 3), energy.reshape(1)
 
 
 def solution(mesh):

time: 62.3 us -> 60.4 us (0.970)
  Pallas kernels: 58.3 us -> 56.4 us
  other arithmetic: 0 us -> 1.42 us
  local copies, waits for them, and re-layouts: 1.42 us -> 0 us
    pallas_call x1, Pallas kernels: 58.3 us -> 56.4 us  [on_device(): pl.pallas_call(functools.partial(pair_kernel, size, nt), out_shape=(jax.S...]
    neg x0 -> x1, other arithmetic: none -> 1.42 us  [on_device(): return (-jnp.swapaxes(forces, 2, 3), energy.reshape(1))]
    unnamed x1 -> x0, local copies, waits for them, and re-layouts: 1.42 us -> none
where the time goes in v5:
time: 60.4 us; the launch traced here: 60.2 us
  Pallas kernels  56.4 us (93%)
  between operations  2.38 us (4%)
  other arithmetic  1.42 us (2%)
    pallas_call x1, Pallas kernels, on_device(): pl.pallas_call(functools.partial(pair_kernel, size, nt), out_shape=(jax.S...  56.4 us
    neg x1, other arithmetic, on_device(): return (-jnp.swapaxes(forces, 2, 3), energy.reshape(1))  1.42 us

profile of v5, /device:TPU:0, one launch (start us, length us, event | category | flops | bytes accessed | tf_op | source)
XLA Modules:
  0.0 60.2 jit_solution(17172763914986148037)
XLA Ops:
  0.6 56.4 %shard_map.77 = (f32[1,4,3,8,128]{4,3,2,1,0:T(8,128)}, f32[1,1]{1,0:T(1,128)}) custom-call(f32[1,4,3,8,128]{4,3,2,1,0:T(8,128)} %bitcast.4, f32[1,4,8,128]{3,2,1,0:T(8,128)} %charge_ref.1, s32[1,4,8,128]{3,2,1,0:T(8,128)} %type_ref.1, s32[1,4,8]{2,1,0:T(4,128)} %count_ref.1, f32[64,64]{1,0:T(8,128)} %c6_ref.1, f32[64,64]{1,0:T(8,128)} %c12_ref.1), custom_call_target="tpu_custom_call" | custom-call | tf_op jit(solution)/shard_map/pallas_call | solution.py:464
  57.0 1.4 %negate_bitcast_fusion = f32[1,4,8,3,128]{4,2,3,1,0:T(8,128)} fusion(f32[1,4,3,8,128]{4,3,2,1,0:T(8,128)} %get-tuple-element.4), kind=kLoop, calls=%fused_computation | loop fusion | flops 12288 | bytes 98304 | tf_op jit(solution)/shard_map/neg | solution.py:495
